TPU v7x, 32 devices: a 4x4x1 block of a 4x4x8 slice. The times are simulated.
32 devices in a mesh: parts: 1 (over z), col: 4 (over y), row: 4 (over x), sub: 2 (over core).
Axes of the slice: x: 4, y: 4, z: 1, core: 2. Of those that a mesh axis runs over, the one named last changes fastest.
The devices are a block of a 4x4x8 slice.
Arguments:
- edge_dist: float32 [8, 128, 1024], P(('parts', 'row', 'sub'), None, 'col')
Outputs:
- output: float32 [8, 128, 1024], P(('parts', 'row', 'sub'), None, 'col')
All inputs are finite; a program needn't handle non-finite values.
Results may differ from a plain program's by a relative error of at most 0.001.
Values sent between devices are 32-bit elements.
A program may use at most 768 MiB of HBM per device.

v0:
```python
import jax
import jax.numpy as jnp
from jax import lax
from jax.sharding import PartitionSpec as P


def close_block(block_in):
    last_axis = block_in.ndim - 1
    def pivot_step(pivot_idx, current):
        col_vec = lax.dynamic_slice_in_dim(current, pivot_idx, 1, axis=last_axis)
        row_vec = lax.dynamic_slice_in_dim(current, pivot_idx, 1, axis=last_axis - 1)
        return jnp.minimum(current, col_vec + row_vec)
    return lax.fori_loop(0, block_in.shape[-1], pivot_step, block_in)


def min_plus(left_mat, right_mat):
    return jnp.min(jnp.expand_dims(left_mat, -1) + jnp.expand_dims(right_mat, -3), axis=-2)


def solution(mesh):
    row_devs = mesh.shape['row'] * mesh.shape['sub']
    col_devs = mesh.shape['col']
    sub_devs = mesh.shape['sub']
    dist_spec = P(('parts', 'row', 'sub'), None, 'col')

    def local_run(local_dist):
        rows_local, blk_size, cols_width = local_dist.shape
        rounds = rows_local * row_devs
        my_row = lax.axis_index('row') * sub_devs + lax.axis_index('sub')
        my_col = lax.axis_index('col')
        current = local_dist
        for round_idx in range(rounds):
            in_row = my_row == round_idx % row_devs
            in_col = my_col == round_idx % col_devs
            row_pos = round_idx // row_devs
            col_pos = (round_idx // col_devs) * blk_size
            diag_blk = close_block(current[row_pos, :, col_pos:col_pos + blk_size])
            diag_blk = lax.pmin(jnp.where(in_row & in_col, diag_blk, jnp.inf), ('row', 'sub', 'col'))
            row_pan = min_plus(diag_blk, current[row_pos])
            row_pan = lax.pmin(jnp.where(in_row, row_pan, jnp.inf), ('row', 'sub'))
            col_pan = min_plus(current[:, :, col_pos:col_pos + blk_size], diag_blk)
            col_pan = lax.pmin(jnp.where(in_col, col_pan, jnp.inf), 'col')
            current = jnp.minimum(current, min_plus(col_pan, row_pan))
        return current

    return jax.shard_map(local_run, mesh=mesh, in_specs=(dist_spec,), out_specs=dist_spec, check_vma=False)
```

profile of v0, /device:TPU:97, one launch (start us, length us, event | category | flops | bytes accessed | tf_op | source)
XLA Modules:
  0.0 1892.0 jit_solution(63574276172925116)
XLA Ops:
  6.6 0.8 slice_bitcast_fusion.7
  7.4 38.6 %while.104 = (s32[]{:T(128)}, f32[128,128]{1,0:T(8,128)S(1)}, s32[]{:T(128)}) while((s32[]{:T(128)}, f32[128,128]{1,0:T(8,128)S(1)}, s32[]{:T(128)}) %tuple.189), condition=%wide.region_1.0_spmd, body=%wide.region_0.0_spmd.sunk | while | flops 32770 | bytes 134197 | solution.py:13
  46.8 95.1 %all-reduce.25.cloned.1.call-done = f32[128,128]{1,0:T(8,128)} async-done(((f32[128,128]{1,0:T(8,128)}), f32[128,128]{1,0:T(8,128)}) %all-reduce.25.cloned.1.call-update) | async-done | bytes 65552 | tf_op jit(solution)/shard_map/pmin | solution.py:38
  141.9 5.3 add_reduce_fusion.15
  147.2 0.7 broadcast_select_fusion.7
  148.0 0.7 copy-done.1
  148.7 4.1 add_reduce_fusion.23
  153.6 47.0 %all-reduce.29.cloned.1.call-done = f32[128,256]{1,0:T(8,128)} async-done(((f32[128,256]{1,0:T(8,128)}), f32[128,256]{1,0:T(8,128)}) %all-reduce.29.cloned.1.call-update) | async-done | bytes 131088 | tf_op jit(solution)/shard_map/pmin | solution.py:40
  200.6 37.7 %all-reduce.27.cloned.1.call-done = f32[128,128]{1,0:T(8,128)} async-done(((f32[128,128]{1,0:T(8,128)}), f32[128,128]{1,0:T(8,128)}) %all-reduce.27.cloned.1.call-update) | async-done | bytes 65552 | tf_op jit(solution)/shard_map/pmin | solution.py:42
  238.3 5.4 add_reduce_fusion.14
  243.7 38.6 %while.105 = (s32[]{:T(128)}, f32[128,128]{1,0:T(8,128)S(1)}, s32[]{:T(128)}) while((s32[]{:T(128)}, f32[128,128]{1,0:T(8,128)S(1)}, s32[]{:T(128)}) %tuple.192), condition=%wide.region_9.10_spmd, body=%wide.region_8.9_spmd.sunk | while | flops 32770 | bytes 134197 | solution.py:13
  283.1 93.5 %all-reduce.31.cloned.1.call-done = f32[128,128]{1,0:T(8,128)} async-done(((f32[128,128]{1,0:T(8,128)}), f32[128,128]{1,0:T(8,128)}) %all-reduce.31.cloned.1.call-update) | async-done | bytes 65552 | tf_op jit(solution)/shard_map/pmin | solution.py:38
  376.5 5.0 add_reduce_fusion.22
  382.4 4.4 add_reduce_fusion.13
  386.8 0.7 broadcast_select_fusion.6
  387.6 28.9 %all-reduce.33.cloned.1.call-done = f32[128,128]{1,0:T(8,128)} async-done(((f32[128,128]{1,0:T(8,128)}), f32[128,128]{1,0:T(8,128)}) %all-reduce.33.cloned.1.call-update) | async-done | bytes 65552 | tf_op jit(solution)/shard_map/pmin | solution.py:42
  416.5 57.1 %all-reduce.35.cloned.1.call-done = f32[128,256]{1,0:T(8,128)} async-done(((f32[128,256]{1,0:T(8,128)}), f32[128,256]{1,0:T(8,128)}) %all-reduce.35.cloned.1.call-update) | async-done | bytes 131088 | tf_op jit(solution)/shard_map/pmin | solution.py:40
  473.6 5.4 add_reduce_fusion.12
  479.0 38.6 %while.106 = (s32[]{:T(128)}, f32[128,128]{1,0:T(8,128)S(1)}, s32[]{:T(128)}) while((s32[]{:T(128)}, f32[128,128]{1,0:T(8,128)S(1)}, s32[]{:T(128)}) %tuple.195), condition=%wide.region_17.18_spmd, body=%wide.region_16.17_spmd.sunk | while | flops 32770 | bytes 134197 | solution.py:13
  518.4 92.4 %all-reduce.37.cloned.1.call-done = f32[128,128]{1,0:T(8,128)} async-done(((f32[128,128]{1,0:T(8,128)}), f32[128,128]{1,0:T(8,128)}) %all-reduce.37.cloned.1.call-update) | async-done | bytes 65552 | tf_op jit(solution)/shard_map/pmin | solution.py:38
  610.7 5.0 add_reduce_fusion.21
  616.6 4.4 add_reduce_fusion.11
  621.8 28.9 %all-reduce.39.cloned.1.call-done = f32[128,128]{1,0:T(8,128)} async-done(((f32[128,128]{1,0:T(8,128)}), f32[128,128]{1,0:T(8,128)}) %all-reduce.39.cloned.1.call-update) | async-done | bytes 65552 | tf_op jit(solution)/shard_map/pmin | solution.py:42
  650.7 57.2 %all-reduce.41.cloned.1.call-done = f32[128,256]{1,0:T(8,128)} async-done(((f32[128,256]{1,0:T(8,128)}), f32[128,256]{1,0:T(8,128)}) %all-reduce.41.cloned.1.call-update) | async-done | bytes 131088 | tf_op jit(solution)/shard_map/pmin | solution.py:40
  707.9 5.4 add_reduce_fusion.10
  713.4 38.6 %while.107 = (s32[]{:T(128)}, f32[128,128]{1,0:T(8,128)S(1)}, s32[]{:T(128)}) while((s32[]{:T(128)}, f32[128,128]{1,0:T(8,128)S(1)}, s32[]{:T(128)}) %tuple.198), condition=%wide.region_25.26_spmd, body=%wide.region_24.25_spmd.sunk | while | flops 32770 | bytes 134197 | solution.py:13
  752.7 92.4 %all-reduce.43.cloned.1.call-done = f32[128,128]{1,0:T(8,128)} async-done(((f32[128,128]{1,0:T(8,128)}), f32[128,128]{1,0:T(8,128)}) %all-reduce.43.cloned.1.call-update) | async-done | bytes 65552 | tf_op jit(solution)/shard_map/pmin | solution.py:38
  845.1 5.0 add_reduce_fusion.20
  851.0 4.4 add_reduce_fusion.9
  855.5 0.7 broadcast_select_fusion.4
  856.3 28.8 %all-reduce.45.cloned.1.call-done = f32[128,128]{1,0:T(8,128)} async-done(((f32[128,128]{1,0:T(8,128)}), f32[128,128]{1,0:T(8,128)}) %all-reduce.45.cloned.1.call-update) | async-done | bytes 65552 | tf_op jit(solution)/shard_map/pmin | solution.py:42
  885.1 57.1 %all-reduce.47.cloned.1.call-done = f32[128,256]{1,0:T(8,128)} async-done(((f32[128,256]{1,0:T(8,128)}), f32[128,256]{1,0:T(8,128)}) %all-reduce.47.cloned.1.call-update) | async-done | bytes 131088 | tf_op jit(solution)/shard_map/pmin | solution.py:40
  942.1 5.4 add_reduce_fusion.8
  947.6 38.6 %while.108 = (s32[]{:T(128)}, f32[128,128]{1,0:T(8,128)S(1)}, s32[]{:T(128)}) while((s32[]{:T(128)}, f32[128,128]{1,0:T(8,128)S(1)}, s32[]{:T(128)}) %tuple.201), condition=%wide.region_33.34_spmd, body=%wide.region_32.33_spmd.sunk | while | flops 32770 | bytes 134197 | solution.py:13
  986.9 92.4 %all-reduce.49.cloned.1.call-done = f32[128,128]{1,0:T(8,128)} async-done(((f32[128,128]{1,0:T(8,128)}), f32[128,128]{1,0:T(8,128)}) %all-reduce.49.cloned.1.call-update) | async-done | bytes 65552 | tf_op jit(solution)/shard_map/pmin | solution.py:38
  1079.3 5.0 add_reduce_fusion.19
  1085.1 4.4 add_reduce_fusion.7
  1089.6 0.7 broadcast_select_fusion.3
  1090.4 28.9 %all-reduce.51.cloned.1.call-done = f32[128,128]{1,0:T(8,128)} async-done(((f32[128,128]{1,0:T(8,128)}), f32[128,128]{1,0:T(8,128)}) %all-reduce.51.cloned.1.call-update) | async-done | bytes 65552 | tf_op jit(solution)/shard_map/pmin | solution.py:42
  1119.3 57.0 %all-reduce.53.cloned.1.call-done = f32[128,256]{1,0:T(8,128)} async-done(((f32[128,256]{1,0:T(8,128)}), f32[128,256]{1,0:T(8,128)}) %all-reduce.53.cloned.1.call-update) | async-done | bytes 131088 | tf_op jit(solution)/shard_map/pmin | solution.py:40
  1176.3 5.4 add_reduce_fusion.6
  1181.8 38.6 %while.109 = (s32[]{:T(128)}, f32[128,128]{1,0:T(8,128)S(1)}, s32[]{:T(128)}) while((s32[]{:T(128)}, f32[128,128]{1,0:T(8,128)S(1)}, s32[]{:T(128)}) %tuple.204), condition=%wide.region_41.42_spmd, body=%wide.region_40.41_spmd.sunk | while | flops 32770 | bytes 134197 | solution.py:13
  1221.1 92.4 %all-reduce.55.cloned.1.call-done = f32[128,128]{1,0:T(8,128)} async-done(((f32[128,128]{1,0:T(8,128)}), f32[128,128]{1,0:T(8,128)}) %all-reduce.55.cloned.1.call-update) | async-done | bytes 65552 | tf_op jit(solution)/shard_map/pmin | solution.py:38
  1313.5 5.0 add_reduce_fusion.18
  1319.3 4.4 add_reduce_fusion.5
  1324.6 28.9 %all-reduce.57.cloned.1.call-done = f32[128,128]{1,0:T(8,128)} async-done(((f32[128,128]{1,0:T(8,128)}), f32[128,128]{1,0:T(8,128)}) %all-reduce.57.cloned.1.call-update) | async-done | bytes 65552 | tf_op jit(solution)/shard_map/pmin | solution.py:42
  1353.5 57.1 %all-reduce.59.cloned.1.call-done = f32[128,256]{1,0:T(8,128)} async-done(((f32[128,256]{1,0:T(8,128)}), f32[128,256]{1,0:T(8,128)}) %all-reduce.59.cloned.1.call-update) | async-done | bytes 131088 | tf_op jit(solution)/shard_map/pmin | solution.py:40
  1410.5 5.4 add_reduce_fusion.4
  1416.0 38.6 %while.110 = (s32[]{:T(128)}, f32[128,128]{1,0:T(8,128)S(1)}, s32[]{:T(128)}) while((s32[]{:T(128)}, f32[128,128]{1,0:T(8,128)S(1)}, s32[]{:T(128)}) %tuple.207), condition=%wide.region_49.50_spmd, body=%wide.region_48.49_spmd.sunk | while | flops 32770 | bytes 134197 | solution.py:13
  1455.3 92.4 %all-reduce.61.cloned.1.call-done = f32[128,128]{1,0:T(8,128)} async-done(((f32[128,128]{1,0:T(8,128)}), f32[128,128]{1,0:T(8,128)}) %all-reduce.61.cloned.1.call-update) | async-done | bytes 65552 | tf_op jit(solution)/shard_map/pmin | solution.py:38
  1547.7 5.0 add_reduce_fusion.17
  1553.5 4.4 add_reduce_fusion.3
  1558.0 0.7 broadcast_select_fusion.1
  1559.0 28.7 %all-reduce.63.cloned.1.call-done = f32[128,128]{1,0:T(8,128)} async-done(((f32[128,128]{1,0:T(8,128)}), f32[128,128]{1,0:T(8,128)}) %all-reduce.63.cloned.1.call-update) | async-done | bytes 65552 | tf_op jit(solution)/shard_map/pmin | solution.py:42
  1587.7 57.2 %all-reduce.65.cloned.1.call-done = f32[128,256]{1,0:T(8,128)} async-done(((f32[128,256]{1,0:T(8,128)}), f32[128,256]{1,0:T(8,128)}) %all-reduce.65.cloned.1.call-update) | async-done | bytes 131088 | tf_op jit(solution)/shard_map/pmin | solution.py:40
  1644.9 5.4 add_reduce_fusion.2
  1650.3 38.6 %while.111 = (s32[]{:T(128)}, f32[128,128]{1,0:T(8,128)S(1)}, s32[]{:T(128)}) while((s32[]{:T(128)}, f32[128,128]{1,0:T(8,128)S(1)}, s32[]{:T(128)}) %tuple.210), condition=%wide.region_57.58_spmd, body=%wide.region_56.57_spmd.sunk | while | flops 32770 | bytes 134197 | solution.py:13
  1689.7 92.4 %all-reduce.67.cloned.1.call-done = f32[128,128]{1,0:T(8,128)} async-done(((f32[128,128]{1,0:T(8,128)}), f32[128,128]{1,0:T(8,128)}) %all-reduce.67.cloned.1.call-update) | async-done | bytes 65552 | tf_op jit(solution)/shard_map/pmin | solution.py:38
  1782.1 5.0 add_reduce_fusion.16
  1787.9 4.4 add_reduce_fusion.1
  1793.0 29.0 %all-reduce.69.cloned.1.call-done = f32[128,128]{1,0:T(8,128)} async-done(((f32[128,128]{1,0:T(8,128)}), f32[128,128]{1,0:T(8,128)}) %all-reduce.69.cloned.1.call-update) | async-done | bytes 65552 | tf_op jit(solution)/shard_map/pmin | solution.py:42
  1822.1 57.1 %all-reduce.71.cloned.1.call-done = f32[128,256]{1,0:T(8,128)} async-done(((f32[128,256]{1,0:T(8,128)}), f32[128,256]{1,0:T(8,128)}) %all-reduce.71.cloned.1.call-update) | async-done | bytes 131088 | tf_op jit(solution)/shard_map/pmin | solution.py:40
  1879.1 5.4 add_reduce_fusion
  1884.5 0.7 bitcast_minimum_fusion
  (3178 shorter events, 289.2 us)
Async XLA Ops:
  6.5 135.3 %all-reduce.25.cloned.1.call-start = ((), (), s32[]{:S(2)}) async-start(), calls=%async_computation | async-start | bytes 131072 | tf_op jit(solution)/shard_map/pmin | solution.py:38
  46.0 95.9 %copy-start = (f32[1,128,256]{2,1,0:T(8,128)S(1)}, f32[1,128,256]{2,1,0:T(8,128)}, u32[]{:S(2)}) copy-start(f32[1,128,256]{2,1,0:T(8,128)} %param.17) | copy-start | bytes 393220
  46.7 153.8 %all-reduce.29.cloned.1.call-start = ((), (), s32[]{:S(2)}) async-start(), calls=%async_computation.2 | async-start | bytes 262144 | tf_op jit(solution)/shard_map/pmin | solution.py:40
  147.9 0.8 copy-start.1
  147.9 90.3 %all-reduce.27.cloned.1.call-start = ((), (), s32[]{:S(2)}) async-start(), calls=%async_computation.1 | async-start | bytes 131072 | tf_op jit(solution)/shard_map/pmin | solution.py:42
  153.5 223.0 %all-reduce.31.cloned.1.call-start = ((), (), s32[]{:S(2)}) async-start(), calls=%async_computation.3 | async-start | bytes 131072 | tf_op jit(solution)/shard_map/pmin | solution.py:38
  283.0 133.5 %all-reduce.33.cloned.1.call-start = ((), (), s32[]{:S(2)}) async-start(), calls=%async_computation.4 | async-start | bytes 131072 | tf_op jit(solution)/shard_map/pmin | solution.py:42
  381.5 0.8 copy-start.6
  382.2 91.4 %all-reduce.35.cloned.1.call-start = ((), (), s32[]{:S(2)}) async-start(), calls=%async_computation.5 | async-start | bytes 262144 | tf_op jit(solution)/shard_map/pmin | solution.py:40
  387.5 223.2 %all-reduce.37.cloned.1.call-start = ((), (), s32[]{:S(2)}) async-start(), calls=%async_computation.6 | async-start | bytes 131072 | tf_op jit(solution)/shard_map/pmin | solution.py:38
  518.3 132.4 %all-reduce.39.cloned.1.call-start = ((), (), s32[]{:S(2)}) async-start(), calls=%async_computation.7 | async-start | bytes 131072 | tf_op jit(solution)/shard_map/pmin | solution.py:42
  615.7 0.8 copy-start.7
  616.4 91.5 %all-reduce.41.cloned.1.call-start = ((), (), s32[]{:S(2)}) async-start(), calls=%async_computation.8 | async-start | bytes 262144 | tf_op jit(solution)/shard_map/pmin | solution.py:40
  621.7 223.4 %all-reduce.43.cloned.1.call-start = ((), (), s32[]{:S(2)}) async-start(), calls=%async_computation.9 | async-start | bytes 131072 | tf_op jit(solution)/shard_map/pmin | solution.py:38
  752.7 132.4 %all-reduce.45.cloned.1.call-start = ((), (), s32[]{:S(2)}) async-start(), calls=%async_computation.10 | async-start | bytes 131072 | tf_op jit(solution)/shard_map/pmin | solution.py:42
  850.1 1.0 copy-start.8
  850.8 91.4 %all-reduce.47.cloned.1.call-start = ((), (), s32[]{:S(2)}) async-start(), calls=%async_computation.11 | async-start | bytes 262144 | tf_op jit(solution)/shard_map/pmin | solution.py:40
  856.2 223.1 %all-reduce.49.cloned.1.call-start = ((), (), s32[]{:S(2)}) async-start(), calls=%async_computation.12 | async-start | bytes 131072 | tf_op jit(solution)/shard_map/pmin | solution.py:38
  986.9 132.4 %all-reduce.51.cloned.1.call-start = ((), (), s32[]{:S(2)}) async-start(), calls=%async_computation.13 | async-start | bytes 131072 | tf_op jit(solution)/shard_map/pmin | solution.py:42
  1084.3 0.8 copy-start.2
  1085.0 91.4 %all-reduce.53.cloned.1.call-start = ((), (), s32[]{:S(2)}) async-start(), calls=%async_computation.14 | async-start | bytes 262144 | tf_op jit(solution)/shard_map/pmin | solution.py:40
  1090.3 223.2 %all-reduce.55.cloned.1.call-start = ((), (), s32[]{:S(2)}) async-start(), calls=%async_computation.15 | async-start | bytes 131072 | tf_op jit(solution)/shard_map/pmin | solution.py:38
  1221.1 132.4 %all-reduce.57.cloned.1.call-start = ((), (), s32[]{:S(2)}) async-start(), calls=%async_computation.16 | async-start | bytes 131072 | tf_op jit(solution)/shard_map/pmin | solution.py:42
  1318.5 0.8 copy-start.3
  1319.2 91.4 %all-reduce.59.cloned.1.call-start = ((), (), s32[]{:S(2)}) async-start(), calls=%async_computation.17 | async-start | bytes 262144 | tf_op jit(solution)/shard_map/pmin | solution.py:40
  1324.5 223.2 %all-reduce.61.cloned.1.call-start = ((), (), s32[]{:S(2)}) async-start(), calls=%async_computation.18 | async-start | bytes 131072 | tf_op jit(solution)/shard_map/pmin | solution.py:38
  1455.3 132.4 %all-reduce.63.cloned.1.call-start = ((), (), s32[]{:S(2)}) async-start(), calls=%async_computation.19 | async-start | bytes 131072 | tf_op jit(solution)/shard_map/pmin | solution.py:42
  1552.7 0.8 copy-start.4
  1553.4 91.5 %all-reduce.65.cloned.1.call-start = ((), (), s32[]{:S(2)}) async-start(), calls=%async_computation.20 | async-start | bytes 262144 | tf_op jit(solution)/shard_map/pmin | solution.py:40
  1558.7 223.4 %all-reduce.67.cloned.1.call-start = ((), (), s32[]{:S(2)}) async-start(), calls=%async_computation.21 | async-start | bytes 131072 | tf_op jit(solution)/shard_map/pmin | solution.py:38
  1689.6 132.4 %all-reduce.69.cloned.1.call-start = ((), (), s32[]{:S(2)}) async-start(), calls=%async_computation.22 | async-start | bytes 131072 | tf_op jit(solution)/shard_map/pmin | solution.py:42
  1787.0 0.8 copy-start.5
  1787.7 91.4 %all-reduce.71.cloned.1.call-start = ((), (), s32[]{:S(2)}) async-start(), calls=%async_computation.23 | async-start | bytes 262144 | tf_op jit(solution)/shard_map/pmin | solution.py:40
Sparse Core Ops, SparseCore 0:
  46.9 94.9 all-reduce.24
  148.0 52.4 all-reduce.28
  202.9 35.3 all-reduce.26
  283.1 93.3 all-reduce.30
  382.3 34.1 all-reduce.32
  418.7 54.8 all-reduce.34
  518.4 92.2 all-reduce.36
  616.5 34.1 all-reduce.38
  653.1 54.8 all-reduce.40
  752.8 92.2 all-reduce.42
  850.9 34.1 all-reduce.44
  887.3 54.8 all-reduce.46
  987.0 92.2 all-reduce.48
  1085.1 34.1 all-reduce.50
  1121.5 54.8 all-reduce.52
  1221.2 92.2 all-reduce.54
  1319.3 34.1 all-reduce.56
  1355.7 54.8 all-reduce.58
  1455.4 92.2 all-reduce.60
  1553.5 34.1 all-reduce.62
  1590.0 54.8 all-reduce.64
  1689.8 92.2 all-reduce.66
  1787.9 34.1 all-reduce.68
  1824.2 54.8 all-reduce.70
where the time goes:
time: 1900 us; the launch traced here: 1890 us
  waiting for transfers between devices  1430 us (75%)
  other arithmetic  218 us (11%)
  local copies, waits for them, and re-layouts  191 us (10%)
  loops' own time  35.6 us (2%)
    pmin x8, waiting for transfers between devices, local_run(): lax.pmin(jnp.where(in_row & in_col, diag_blk, jnp.inf), ('row', 'sub', 'c...  743 us
    pmin x8, waiting for transfers between devices, local_run(): row_pan = lax.pmin(jnp.where(in_row, row_pan, jnp.inf), ('row', 'sub'))  447 us
    pmin x8, waiting for transfers between devices, local_run(): col_pan = lax.pmin(jnp.where(in_col, col_pan, jnp.inf), 'col')  240 us
    dynamic_slice x1024, local copies, waits for them, and re-layouts, pivot_step(): col_vec = lax.dynamic_slice_in_dim(current, pivot_idx, 1, axis=last_axis)  177 us
    reduce_min x24, other arithmetic, min_plus(): jnp.min(jnp.expand_dims(left_mat, -1) + jnp.expand_dims(right_mat, -3), a...  118 us
    min x1024, other arithmetic, pivot_step(): return jnp.minimum(current, col_vec + row_vec)  84.1 us
  transfers between devices with their start and end apart: 24, of which 24 were waited for; matrix products, arithmetic and copies ran while one was open for 2% of the time, Pallas kernels for 0%

commit v1 on v0

v1 whole, which is shorter than its diff:
```python
import functools

import jax
import jax.numpy as jnp
from jax import lax
from jax.experimental import pallas as pl
from jax.experimental.pallas import tpu as pltpu
from jax.sharding import PartitionSpec as P

SUBL = 8
LANES = 128
CHUNK = 32


def relax(acc, src, lanes, rows):
    for n, lane in enumerate(lanes):
        acc = jnp.minimum(acc, jnp.broadcast_to(src[:, lane:lane + 1], acc.shape) + jnp.broadcast_to(rows(n), acc.shape))
    return acc


def close_tile(tile, piv_cols):
    wide = jnp.concatenate([jnp.broadcast_to(piv_cols[:, l:l + 1], (SUBL, LANES)) for l in range(SUBL)] + [tile], axis=1)
    for p in range(SUBL):
        piv, wide = wide[:, :LANES], wide[:, LANES:]
        reps = wide.shape[1] // LANES
        wide = jnp.minimum(wide, jnp.concatenate([piv] * reps, axis=1) + jnp.broadcast_to(wide[p:p + 1, :], wide.shape))
    return wide


def kernel(nrows, ncols, nsub, blk, in_ref, out_ref, work, diag_in, diag_st, colp, colp_st, rowp,
           c_send, c_recv, s_send, s_recv, r_send, r_recv, f_send, n_send, n_recv):
    x = lax.axis_index('row')
    sub = lax.axis_index('sub')
    my_col = lax.axis_index('col')
    nx = nrows // nsub
    my_row = x * nsub + sub
    nchunk = blk // CHUNK
    own = in_ref.shape[2]
    dlo = blk + own
    width = dlo + blk
    tiles = blk // SUBL
    tiles_per_chunk = CHUNK // SUBL

    def dev(row=None, col=None):
        out = {}
        if row is not None:
            out['row'] = row // nsub
            out['sub'] = row % nsub
        if col is not None:
            out['col'] = col
        return out

    def signal(target):
        pl.semaphore_signal(barrier, inc=1, device_id=target, device_id_type=pl.DeviceIdType.MESH)

    barrier = pltpu.get_barrier_semaphore()
    for d in range(1, ncols):
        signal(dev(col=(my_col + d) % ncols))
    for d in range(1, nrows):
        signal(dev(row=(my_row + d) % nrows))
    for dr in (1, nrows - 1):
        for d in range(1, ncols):
            signal(dev((my_row + dr) % nrows, (my_col + d) % ncols))
    work[:, blk:dlo] = in_ref[0]
    pl.semaphore_wait(barrier, 3 * (ncols - 1) + nrows - 1)

    def remote(src, dst, ssem, rsem, target):
        return pltpu.make_async_remote_copy(src_ref=src, dst_ref=dst, send_sem=ssem, recv_sem=rsem,
                                            device_id=target, device_id_type=pl.DeviceIdType.MESH)

    def col_copy(k, d):
        return remote(colp_st.at[k], colp.at[k], c_send.at[k, d - 1], c_recv.at[k], dev(col=(my_col + d) % ncols))

    def diag_copy(d):
        return remote(diag_st, diag_in, s_send.at[d - 1], s_recv.at[0], dev(col=(my_col + d) % ncols))

    def panel(k, a):
        lo = blk if a == nchunk - 1 else 0
        return rowp.at[k, a, :, lo:dlo]

    def row_copy(k, a, d):
        target = {'sub': (sub + 1) % nsub} if d == 0 else {'row': (x + d) % nx, 'sub': 0}
        return remote(panel(k, a), panel(k, a), r_send.at[a, d], r_recv.at[k, a], target)

    def fwd_copy(k, a):
        return remote(panel(k, a), panel(k, a), f_send.at[k, a], r_recv.at[k, a], {'sub': (sub + 1) % nsub})

    def nxt_copy(k, a, d):
        src = pl.ds(pl.multiple_of(blk + (k + 1) // ncols * blk, LANES), blk)
        return remote(rowp.at[k, a, :, src], rowp.at[k, a, :, dlo:width], n_send.at[a, d], n_recv.at[a],
                      dev(k + 1, (my_col + d) % ncols))

    def own_block(b):
        return work[:, pl.ds(pl.multiple_of(blk + b // ncols * blk, LANES), blk)]

    def send_col(k):
        @pl.when((my_col == k % ncols) & (my_row != k))
        def _():
            block = own_block(k)
            colp[k] = block
            colp_st[k] = block
            for d in range(1, ncols):
                col_copy(k, d).start()

    def send_diag():
        block = own_block(my_row)
        work[:, dlo:width] = block
        diag_st[...] = block
        for d in range(1, ncols):
            diag_copy(d).start()

    def recv_diag():
        @pl.when(my_col != my_row % ncols)
        def _():
            diag_copy(1).wait_recv()
            work[:, dlo:width] = diag_in[...]

    @pl.when((my_row <= 1) & (my_col == my_row % ncols))
    def _():
        send_diag()
    send_col(0)

    def apply_rows(lo, hi, lane_lo, k, a, count, step):
        def body(it, carry):
            r = pl.ds(pl.multiple_of(it * step, step), step)
            rows = lambda n: rowp[k, a, n:n + 1, lo:hi]
            src = work[r, lane_lo:lane_lo + blk]
            work[r, lo:hi] = relax(work[r, lo:hi], src, [a * CHUNK + l for l in range(CHUNK)], rows)
            return carry
        lax.fori_loop(0, count // step, body, 0)

    def own_turn(k):
        lo, hi, dl = blk, width, dlo - blk
        load = lambda t, n=1: work[t * SUBL:(t + n) * SUBL, lo:hi]
        piv = lambda v, g: v[:, dl + g * SUBL:dl + (g + 1) * SUBL]
        cur = close_tile(load(0), piv(load(0), 0))
        for g in range(tiles):
            a = g // tiles_per_chunk
            rows = lambda n: cur[n:n + 1, :]
            if g + 1 < tiles:
                nxt = load(g + 1)
                nxt = relax(nxt, piv(nxt, g), range(SUBL), rows)
                nxt = close_tile(nxt, piv(nxt, g + 1))
            spans = [(a * tiles_per_chunk, g), (g + 2, tiles)]
            for first, last in spans:
                for t in range(first, last, 4):
                    n = min(4, last - t)
                    vals = load(t, n)
                    work[t * SUBL:(t + n) * SUBL, lo:hi] = relax(vals, piv(vals, g), range(SUBL), rows)
            work[g * SUBL:(g + 1) * SUBL, lo:hi] = cur
            if g + 1 < tiles:
                cur = nxt
            if (g + 1) % tiles_per_chunk == 0:
                r = slice(a * CHUNK, (a + 1) * CHUNK)
                rowp[k, a, :, 0:blk] = work[r, dlo:width]
                rowp[k, a, :, blk:dlo] = work[r, blk:dlo]
                rowp[k, a, :, dlo:width] = work[r, dlo:width]
                @pl.when((k + 1 < nrows) & (my_col == (k + 1) % ncols))
                def _():
                    for d in (1, 0) + tuple(range(ncols - 1, 1, -1)):
                        nxt_copy(k, a, d).start()
                for d in (1, 0, nx - 1) + tuple(range(2, nx - 1)):
                    row_copy(k, a, d).start()
        for a in range(1, nchunk):
            apply_rows(blk, width, dlo, k, a, a * CHUNK, CHUNK)

    def other_turn(k, is_next):
        for a in range(nchunk):
            fwd_copy(k, a).wait_recv()

            @pl.when((sub == 0) & (x != k // nsub))
            def _():
                fwd_copy(k, a).start()
            if is_next:
                nxt_copy(k, a, 0).wait_recv()
            apply_rows(0 if a < nchunk - 1 else blk, width if is_next else dlo, 0, k, a, blk, 64)

    def round_body(k, carry):
        @pl.when(my_row == k)
        def _():
            @pl.when(k == 0)
            def _():
                recv_diag()
            own_turn(k)

        @pl.when(my_row != k)
        def _():
            @pl.when(my_col != k % ncols)
            def _():
                col_copy(k, 1).wait_recv()
            work[:, 0:blk] = colp[k]

            @pl.when(my_row == k + 1)
            def _():
                recv_diag()
                other_turn(k, True)

            @pl.when(my_row != k + 1)
            def _():
                other_turn(k, False)

        @pl.when(k + 1 < nrows)
        def _():
            send_col(k + 1)

        @pl.when((my_row == k + 2) & (my_col == my_row % ncols))
        def _():
            send_diag()
        return carry

    lax.fori_loop(0, nrows, round_body, 0)

    out_ref[0] = work[:, blk:dlo]

    @pl.when(my_col == my_row % ncols)
    def _():
        for d in range(1, ncols):
            diag_copy(d).wait_send()

    def drain(k, carry):
        @pl.when((my_col == k % ncols) & (my_row != k))
        def _():
            for d in range(1, ncols):
                col_copy(k, d).wait_send()

        @pl.when((sub == 0) & (x != k // nsub))
        def _():
            for a in range(nchunk):
                fwd_copy(k, a).wait_send()
        return carry
    lax.fori_loop(0, nrows, drain, 0)
    for a in range(nchunk):
        for d in range(nx):
            row_copy(my_row, a, d).wait_send()

    @pl.when((my_row + 1 < nrows) & (my_col == (my_row + 1) % ncols))
    def _():
        for a in range(nchunk):
            for d in range(ncols):
                nxt_copy(my_row, a, d).wait_send()


def solution(mesh):
    nsub = mesh.shape['sub']
    nrows = mesh.shape['row'] * nsub
    ncols = mesh.shape['col']
    dist_spec = P(('parts', 'row', 'sub'), None, 'col')

    def local_run(local):
        rows_local, blk, own = local.shape
        assert rows_local == 1
        nchunk = blk // CHUNK
        nx = nrows // nsub
        dma = pltpu.SemaphoreType.DMA
        vmem = lambda *s: pltpu.VMEM(s, jnp.float32)
        return pl.pallas_call(
            functools.partial(kernel, nrows, ncols, nsub, blk),
            out_shape=jax.ShapeDtypeStruct(local.shape, local.dtype),
            in_specs=[pl.BlockSpec(memory_space=pltpu.VMEM)],
            out_specs=pl.BlockSpec(memory_space=pltpu.VMEM),
            scratch_shapes=[
                vmem(blk, own + 2 * blk), vmem(blk, blk), vmem(blk, blk),
                vmem(nrows, blk, blk), vmem(nrows, blk, blk),
                vmem(nrows, nchunk, CHUNK, own + 2 * blk),
                dma((nrows, ncols - 1)), dma((nrows,)), dma((ncols - 1,)), dma((1,)),
                dma((nchunk, nx)), dma((nrows, nchunk)), dma((nrows, nchunk)),
                dma((nchunk, ncols)), dma((nchunk,)),
            ],
            compiler_params=pltpu.CompilerParams(collective_id=0, has_side_effects=True),
        )(local)

    return jax.shard_map(local_run, mesh=mesh, in_specs=(dist_spec,), out_specs=dist_spec, check_vma=False)
```

time: 1900 us -> 86.5 us (0.05)
  waiting for transfers between devices: 1430 us -> 0 us
  other arithmetic: 218 us -> 0 us
  local copies, waits for them, and re-layouts: 191 us -> 1.57 us
  Pallas kernels: 0 us -> 84.8 us
  loops' own time: 35.6 us -> 0 us
    pmin x24 -> x0, waiting for transfers between devices: 1430 us -> none  [the longest x8 743 us: local_run(): lax.pmin(jnp.where(in_row & in_col, diag_blk, jnp.inf), ('row', 'sub', 'c...]
    dynamic_slice x1024 -> x0, local copies, waits for them, and re-layouts: 177 us -> none  [pivot_step(): col_vec = lax.dynamic_slice_in_dim(current, pivot_idx, 1, axis=last_axis)]
    reduce_min x24 -> x0, other arithmetic: 118 us -> none  [min_plus(): jnp.min(jnp.expand_dims(left_mat, -1) + jnp.expand_dims(right_mat, -3), a...]
    min x1032 -> x0, other arithmetic: 84.9 us -> none  [the longest x1024 84.1 us: pivot_step(): return jnp.minimum(current, col_vec + row_vec)]
    pallas_call x0 -> x1, Pallas kernels: none -> 84.8 us  [local_run(): pl.pallas_call(functools.partial(kernel, nrows, ncols, nsub, blk), out_sh...]
    another operation x8 -> x0, loops' own time: 35.6 us -> none  [close_block(): return lax.fori_loop(0, block_in.shape[-1], pivot_step, block_in)]
  transfers between devices with their start and end apart: 24 -> 0, of which waited for: 24 -> 0; matrix products, arithmetic and copies ran while one was open for 2% -> 0% of each run, Pallas kernels for 0% -> 0%
where the time goes in v1:
time: 86.5 us; the launch traced here: 86.4 us
  Pallas kernels  84.8 us (98%)
  local copies, waits for them, and re-layouts  1.57 us (2%)
    pallas_call x1, Pallas kernels, local_run(): pl.pallas_call(functools.partial(kernel, nrows, ncols, nsub, blk), out_sh...  84.8 us

profile of v1, /device:TPU:97, one launch (start us, length us, event | category | flops | bytes accessed | tf_op | source)
XLA Modules:
  0.0 86.4 jit_solution(8151922977739154868)
XLA Ops:
  0.0 84.8 %shard_map.17 = f32[1,128,256]{2,1,0:T(8,128)} custom-call(f32[1,128,256]{2,1,0:T(8,128)} %in_ref.1), custom_call_target="tpu_custom_call" | custom-call | tf_op jit(solution)/shard_map/pallas_call | solution.py:256
  84.8 1.6 %copy.3 = f32[1,128,256]{2,1,0:T(8,128)} copy(f32[1,128,256]{2,1,0:T(8,128)} %shard_map.17) | data formatting | bytes 262144

commit v2 on v1

v2 whole, which is shorter than its diff:
```python
import functools

import jax
import jax.numpy as jnp
from jax import lax
from jax.experimental import pallas as pl
from jax.experimental.pallas import tpu as pltpu
from jax.sharding import PartitionSpec as P

SUBL = 8
LANES = 128
CHUNK = 32
HALVES = 2


def relax(acc, src, cols, rows):
    for n, lane in enumerate(cols):
        acc = jnp.minimum(acc, jnp.broadcast_to(src[:, lane:lane + 1], acc.shape) + jnp.broadcast_to(rows(n), acc.shape))
    return acc


def lane_bcast(tile, lane):
    return jnp.broadcast_to(tile[:, lane:lane + 1], (tile.shape[0], LANES))


def widen(x, width):
    return jnp.concatenate([x] * (width // LANES), axis=1)


def close_tile(tile, base):
    wide = jnp.concatenate([lane_bcast(tile, base + l) for l in range(SUBL)] + [tile], axis=1)
    for p in range(SUBL):
        piv, wide = wide[:, :LANES], wide[:, LANES:]
        wide = jnp.minimum(wide, widen(piv, wide.shape[1]) + jnp.broadcast_to(wide[p:p + 1, :], wide.shape))
    return wide


def kernel(nrows, ncols, nsub, blk, in_ref, out_ref, work, diag_in, colp, rowp, lanes, spread, io_sem,
           c_send, c_recv, s_send, s_recv, r_send, r_recv, f_send, n_send, n_recv):
    x = lax.axis_index('row')
    sub = lax.axis_index('sub')
    my_col = lax.axis_index('col')
    nx = nrows // nsub
    my_row = x * nsub + sub
    nchunk = blk // CHUNK
    half = blk // HALVES
    own = in_ref.shape[2]
    dlo = blk + own
    width = dlo + blk
    tiles = blk // SUBL
    tiles_per_chunk = CHUNK // SUBL

    def dev(row=None, col=None):
        out = {}
        if row is not None:
            out['row'] = row // nsub
            out['sub'] = row % nsub
        if col is not None:
            out['col'] = col
        return out

    def signal(target):
        pl.semaphore_signal(barrier, inc=1, device_id=target, device_id_type=pl.DeviceIdType.MESH)

    load_in = pltpu.make_async_copy(in_ref.at[0], work.at[:, blk:dlo], io_sem.at[0])
    load_in.start()
    barrier = pltpu.get_barrier_semaphore()
    for d in range(1, ncols):
        signal(dev(col=(my_col + d) % ncols))
    for d in range(1, nrows):
        signal(dev(row=(my_row + d) % nrows))
    for dr in (1, nrows - 1):
        for d in range(1, ncols):
            signal(dev((my_row + dr) % nrows, (my_col + d) % ncols))
    load_in.wait()
    pl.semaphore_wait(barrier, 3 * (ncols - 1) + nrows - 1)

    def remote(src, dst, ssem, rsem, target):
        return pltpu.make_async_remote_copy(src_ref=src, dst_ref=dst, send_sem=ssem, recv_sem=rsem,
                                            device_id=target, device_id_type=pl.DeviceIdType.MESH)

    def half_rows(h):
        return pl.ds(pl.multiple_of(h * half, half), half)

    def col_copy(k, h, d, n):
        part = colp.at[k, half_rows(h)]
        return remote(part, part, c_send.at[k, h, n], c_recv.at[k, h], dev(col=(my_col + d) % ncols))

    def diag_copy(h, d):
        part = diag_in.at[half_rows(h)]
        return remote(part, part, s_send.at[h, d - 1], s_recv.at[h], dev(col=(my_col + d) % ncols))

    def panel(k, a):
        lo = blk if a == nchunk - 1 else 0
        return rowp.at[k, a, :, lo:dlo]

    def row_copy(k, a, n):
        target = {'sub': (sub + 1) % nsub} if n == 0 else {'row': (x + (nx - 1, 1)[n - 1]) % nx, 'sub': 0}
        return remote(panel(k, a), panel(k, a), r_send.at[a, n], r_recv.at[k, a], target)

    def fwd_copy(k, a):
        return remote(panel(k, a), panel(k, a), f_send.at[k, a, 0], r_recv.at[k, a], {'sub': (sub + 1) % nsub})

    def far_step(a):
        return 1 if a % 2 == 0 else nx - 1

    def far_copy(k, a):
        return remote(panel(k, a), panel(k, a), f_send.at[k, a, 1], r_recv.at[k, a], {'row': (x + far_step(a)) % nx, 'sub': 0})

    def fwd_here(k):
        return (sub == 0) & (x != k // nsub)

    def far_here(k, a):
        return (sub == 0) & (x == (k // nsub + far_step(a)) % nx)

    def nxt_copy(k, a, d):
        src = pl.ds(pl.multiple_of(blk + (k + 1) // ncols * blk, LANES), blk)
        return remote(rowp.at[k, a, :, src], rowp.at[k, a, :, dlo:width], n_send.at[a, d - 1], n_recv.at[a],
                      dev(k + 1, (my_col + d) % ncols))

    def own_cols(b):
        return pl.ds(pl.multiple_of(blk + b // ncols * blk, LANES), blk)

    def send_col(k, h):
        colp[k, half_rows(h)] = work[half_rows(h), own_cols(k)]
        for d in (1, ncols - 1) + tuple(range(2, ncols - 1)):
            col_copy(k, h, d, d - 1).start()

    def send_diag(h):
        diag_in[half_rows(h)] = work[half_rows(h), own_cols(my_row)]
        work[half_rows(h), dlo:width] = diag_in[half_rows(h)]
        for d in range(1, ncols):
            diag_copy(h, d).start()

    def recv_diag():
        @pl.when(my_col != my_row % ncols)
        def _():
            for h in range(HALVES):
                diag_copy(h, 1).wait_recv()
            work[:, dlo:width] = diag_in[...]

    def recv_col(k, h):
        @pl.when(my_col != k % ncols)
        def _():
            col_copy(k, h, 1, 0).wait_recv()
        work[half_rows(h), 0:blk] = colp[k, half_rows(h)]

    @pl.when((my_row <= 1) & (my_col == my_row % ncols))
    def _():
        for h in range(HALVES):
            send_diag(h)

    @pl.when((my_row != 0) & (my_col == 0))
    def _():
        for h in range(HALVES):
            send_col(0, h)

    def apply_rows(lo, hi, lane_lo, k, a, count, step):
        def body(it, carry):
            r = pl.ds(pl.multiple_of(it * step, step), step)
            rows = lambda n: rowp[k, a, n:n + 1, lo:hi]
            src = work[r, lane_lo:lane_lo + blk]
            work[r, lo:hi] = relax(work[r, lo:hi], src, [a * CHUNK + l for l in range(CHUNK)], rows)
            return carry
        lax.fori_loop(0, count // step, body, 0)

    def own_turn(k):
        lo, hi, dl = blk, width, dlo - blk

        def rows(f, l):
            return slice(f * SUBL, l * SUBL)

        def in_play(g):
            return range(g // tiles_per_chunk * tiles_per_chunk, tiles) if g < tiles else range(0)

        def runs(ts):
            out = []
            for t in ts:
                if out and out[-1][1] == t and t - out[-1][0] < 4:
                    out[-1][1] = t + 1
                else:
                    out.append([t, t + 1])
            return out

        def expand(g, f, l, vals):
            for n in range(SUBL):
                lanes[g % 2, n, rows(f, l), :] = lane_bcast(vals, dl + g * SUBL + n)

        def relaxed(g, f, l, cur):
            acc = work[rows(f, l), lo:hi]
            for n in range(SUBL):
                acc = jnp.minimum(acc, widen(lanes[g % 2, n, rows(f, l), :], hi - lo) + jnp.broadcast_to(cur[n:n + 1, :], acc.shape))
            return acc

        def relax_tiles(g, ts, cur):
            for f, l in runs(ts):
                vals = relaxed(g, f, l, cur)
                work[rows(f, l), lo:hi] = vals
                if f in in_play(g + 1):
                    expand(g + 1, f, l, vals)

        work[rows(0, 1), lo:hi] = close_tile(work[rows(0, 1), lo:hi], dl)
        for f, l in runs(range(1, tiles)):
            expand(0, f, l, work[rows(f, l), lo:hi])
        for g in range(tiles):
            a = g // tiles_per_chunk
            cur = work[rows(g, g + 1), lo:hi]
            rest = [t for t in in_play(g) if t not in (g, g + 1)]
            if (g + 1) % tiles_per_chunk == 0:
                relax_tiles(g, [t for t in rest if t < g], cur)
                rest = [t for t in rest if t > g]
                r = slice(a * CHUNK, (a + 1) * CHUNK)
                rowp[k, a, :, 0:blk] = work[r, dlo:width]
                rowp[k, a, :, blk:dlo] = work[r, blk:dlo]
                rowp[k, a, :, dlo:width] = work[r, dlo:width]
                @pl.when((k + 1 < nrows) & (my_col == (k + 1) % ncols))
                def _():
                    nxt_copy(k, a, 1).start()
                row_copy(k, a, 0).start()
                row_copy(k, a, 2).start()
                @pl.when((k + 1 < nrows) & (my_col == (k + 1) % ncols))
                def _():
                    for d in range(2, ncols):
                        nxt_copy(k, a, d).start()
                row_copy(k, a, 1).start()
            if g + 1 < tiles:
                nxt = relaxed(g, g + 1, g + 2, cur)
                wide = jnp.concatenate([lane_bcast(nxt, dl + (g + 1) * SUBL + n) for n in range(SUBL)] + [nxt], axis=1)
                if g in in_play(g + 1):
                    expand(g + 1, g, g + 1, cur)
            relax_tiles(g, rest, cur)
            if g + 1 < tiles:
                for p in range(SUBL):
                    piv, wide = wide[:, :LANES], wide[:, LANES:]
                    wide = jnp.minimum(wide, widen(piv, wide.shape[1]) + jnp.broadcast_to(wide[p:p + 1, :], wide.shape))
                work[rows(g + 1, g + 2), lo:hi] = wide
        for a in range(1, nchunk):
            apply_rows(blk, width, dlo, k, a, a * CHUNK, CHUNK)

    def recv_row(k, a):
        fwd_copy(k, a).wait_recv()

        @pl.when(fwd_here(k))
        def _():
            fwd_copy(k, a).start()

        @pl.when(far_here(k, a))
        def _():
            far_copy(k, a).start()

    def next_turn(k):
        holder = my_col == (k + 1) % ncols
        recv_row(k, 0)
        for h in range(HALVES):
            recv_col(k, h)
        recv_diag()
        for a in range(nchunk):
            if a > 0:
                recv_row(k, a)

            @pl.when(holder)
            def _():
                rowp[k, a, :, dlo:width] = rowp[k, a, :, own_cols(k + 1)]

            @pl.when(jnp.logical_not(holder))
            def _():
                nxt_copy(k, a, 1).wait_recv()
            apply_rows(0 if a < nchunk - 1 else blk, width, 0, k, a, blk, blk)

    def relax_half(k, a, h, sections, save=False, load=False):
        r = half_rows(h)
        accs = [work[r, c] for c in sections]
        src = work[r, 0:blk]
        for n in range(CHUNK):
            if load:
                wide = spread[a * CHUNK + n, r, :]
            else:
                wide = lane_bcast(src, a * CHUNK + n)
            if save:
                spread[a * CHUNK + n, r, :] = wide
            accs = [jnp.minimum(acc, widen(wide, acc.shape[1]) + jnp.broadcast_to(rowp[k, a, n:n + 1, c], acc.shape))
                    for acc, c in zip(accs, sections)]
        for acc, c in zip(accs, sections):
            work[r, c] = acc

    def other_turn(k):
        first = slice(0, blk)
        holder = (k + 1 < nrows) & (my_col == (k + 1) % ncols)
        recv_row(k, 0)

        @pl.when(holder)
        def _():
            def body(h, carry):
                recv_col(k, h)
                for a in range(nchunk):
                    if a > 0:
                        @pl.when(h == 0)
                        def _():
                            recv_row(k, a)
                    secs = [first] if a < nchunk - 1 else []
                    relax_half(k, a, h, secs + [own_cols(k + 1)], save=True)
                send_col(k + 1, h)
                return carry
            lax.fori_loop(0, HALVES, body, 0)

            other = pl.ds(pl.multiple_of(own - (k + 1) // ncols * blk, LANES), blk)
            def rest(h, carry):
                for a in range(nchunk):
                    relax_half(k, a, h, [other], load=True)
                return carry
            lax.fori_loop(0, HALVES, rest, 0)

        @pl.when(jnp.logical_not(holder))
        def _():
            def body(h, carry):
                recv_col(k, h)
                for a in range(nchunk):
                    if a > 0:
                        @pl.when(h == 0)
                        def _():
                            recv_row(k, a)
                    relax_half(k, a, h, [slice(0 if a < nchunk - 1 else blk, dlo)])

                @pl.when((my_row == k + 2) & (my_col == my_row % ncols))
                def _():
                    send_diag(h)
                return carry
            lax.fori_loop(0, HALVES, body, 0)

    def round_body(k, carry):
        @pl.when(my_row == k)
        def _():
            @pl.when(k == 0)
            def _():
                recv_diag()
            own_turn(k)

            @pl.when((k + 1 < nrows) & (my_col == (k + 1) % ncols))
            def _():
                for h in range(HALVES):
                    send_col(k + 1, h)

        @pl.when(my_row == k + 1)
        def _():
            next_turn(k)

        @pl.when((my_row != k) & (my_row != k + 1))
        def _():
            other_turn(k)
        return carry

    lax.fori_loop(0, nrows, round_body, 0)

    store_out = pltpu.make_async_copy(work.at[:, blk:dlo], out_ref.at[0], io_sem.at[0])
    store_out.start()

    @pl.when(my_col == my_row % ncols)
    def _():
        for h in range(HALVES):
            for d in range(1, ncols):
                diag_copy(h, d).wait_send()

    def drain(k, carry):
        @pl.when((my_col == k % ncols) & (my_row != k))
        def _():
            for h in range(HALVES):
                for d in range(1, ncols):
                    col_copy(k, h, d, d - 1).wait_send()
        for a in range(nchunk):
            @pl.when(fwd_here(k))
            def _():
                fwd_copy(k, a).wait_send()

            @pl.when(far_here(k, a))
            def _():
                far_copy(k, a).wait_send()
        return carry
    lax.fori_loop(0, nrows, drain, 0)
    for a in range(nchunk):
        for n in range(nx - 1):
            row_copy(my_row, a, n).wait_send()

        @pl.when((my_row + 1 < nrows) & (my_col == (my_row + 1) % ncols))
        def _():
            for d in range(1, ncols):
                nxt_copy(my_row, a, d).wait_send()
    store_out.wait()


def solution(mesh):
    nsub = mesh.shape['sub']
    nrows = mesh.shape['row'] * nsub
    ncols = mesh.shape['col']
    dist_spec = P(('parts', 'row', 'sub'), None, 'col')

    def local_run(local):
        rows_local, blk, own = local.shape
        assert rows_local == 1
        nchunk = blk // CHUNK
        nx = nrows // nsub
        dma = pltpu.SemaphoreType.DMA
        vmem = lambda *s: pltpu.VMEM(s, jnp.float32)
        return pl.pallas_call(
            functools.partial(kernel, nrows, ncols, nsub, blk),
            out_shape=jax.ShapeDtypeStruct(local.shape, local.dtype),
            in_specs=[pl.BlockSpec(memory_space=pl.ANY)],
            out_specs=pl.BlockSpec(memory_space=pl.ANY),
            scratch_shapes=[
                vmem(blk, own + 2 * blk), vmem(blk, blk), vmem(nrows, blk, blk),
                vmem(nrows, nchunk, CHUNK, own + 2 * blk), vmem(2, SUBL, blk, LANES), vmem(blk, blk, LANES), dma((1,)),
                dma((nrows, HALVES, ncols - 1)), dma((nrows, HALVES)), dma((HALVES, ncols - 1)), dma((HALVES,)),
                dma((nchunk, nx - 1)), dma((nrows, nchunk)), dma((nrows, nchunk, 2)),
                dma((nchunk, ncols - 1)), dma((nchunk,)),
            ],
            compiler_params=pltpu.CompilerParams(collective_id=0, has_side_effects=True),
        )(local)

    return jax.shard_map(local_run, mesh=mesh, in_specs=(dist_spec,), out_specs=dist_spec, check_vma=False)
```

time: 86.5 us -> 83.5 us (0.965)
  the two profiles are of different devices: /device:TPU:97 before, /device:TPU:99 now
where the time goes in v2:
time: 83.5 us; the launch traced here: 83.4 us
  Pallas kernels  81.8 us (98%)
  local copies, waits for them, and re-layouts  1.57 us (2%)
    pallas_call x1, Pallas kernels, local_run(): pl.pallas_call(functools.partial(kernel, nrows, ncols, nsub, blk), out_sh...  81.8 us

profile of v2, /device:TPU:99, one launch (start us, length us, event | category | flops | bytes accessed | tf_op | source)
XLA Modules:
  0.0 83.4 jit_solution(12644504246507493818)
XLA Ops:
  0.0 81.8 %shard_map.17 = f32[1,128,256]{2,1,0:T(8,128)} custom-call(f32[1,128,256]{2,1,0:T(8,128)} %in_ref.1), custom_call_target="tpu_custom_call" | custom-call | tf_op jit(solution)/shard_map/pallas_call | solution.py:403
  81.9 1.6 %copy.3 = f32[1,128,256]{2,1,0:T(8,128)} copy(f32[1,128,256]{2,1,0:T(8,128)} %shard_map.17) | data formatting | bytes 262144

commit v3 on v2

--- a/solution.py
+++ b/solution.py
@@ -11,6 +11,7 @@
 LANES = 128
 CHUNK = 32
 HALVES = 2
+FULL = False
 
 
 def relax(acc, src, cols, rows):
@@ -27,15 +28,7 @@
     return jnp.concatenate([x] * (width // LANES), axis=1)
 
 
-def close_tile(tile, base):
-    wide = jnp.concatenate([lane_bcast(tile, base + l) for l in range(SUBL)] + [tile], axis=1)
-    for p in range(SUBL):
-        piv, wide = wide[:, :LANES], wide[:, LANES:]
-        wide = jnp.minimum(wide, widen(piv, wide.shape[1]) + jnp.broadcast_to(wide[p:p + 1, :], wide.shape))
-    return wide
-
-
-def kernel(nrows, ncols, nsub, blk, in_ref, out_ref, work, diag_in, colp, rowp, lanes, spread, io_sem,
+def kernel(nrows, ncols, nsub, blk, in_ref, out_ref, work, diag_in, colp, rowp, spread, io_sem,
            c_send, c_recv, s_send, s_recv, r_send, r_recv, f_send, n_send, n_recv):
     x = lax.axis_index('row')
     sub = lax.axis_index('sub')
@@ -69,11 +62,14 @@
         signal(dev(col=(my_col + d) % ncols))
     for d in range(1, nrows):
         signal(dev(row=(my_row + d) % nrows))
-    for dr in (1, nrows - 1):
-        for d in range(1, ncols):
-            signal(dev((my_row + dr) % nrows, (my_col + d) % ncols))
+    for step, there in ((1, my_row + 1 < nrows), (-1, my_row > 0)):
+        @pl.when(there)
+        def _():
+            for d in range(1, ncols):
+                signal(dev(my_row + step, (my_col + d) % ncols))
     load_in.wait()
-    pl.semaphore_wait(barrier, 3 * (ncols - 1) + nrows - 1)
+    middle = jnp.where((my_row > 0) & (my_row + 1 < nrows), 1, 0)
+    pl.semaphore_wait(barrier, (2 + middle) * (ncols - 1) + nrows - 1)
 
     def remote(src, dst, ssem, rsem, target):
         return pltpu.make_async_remote_copy(src_ref=src, dst_ref=dst, send_sem=ssem, recv_sem=rsem,
@@ -95,7 +91,7 @@
         return rowp.at[k, a, :, lo:dlo]
 
     def row_copy(k, a, n):
-        target = {'sub': (sub + 1) % nsub} if n == 0 else {'row': (x + (nx - 1, 1)[n - 1]) % nx, 'sub': 0}
+        target = {'sub': (sub + 1) % nsub} if n == 0 else {'row': (x + (nx - 1, 1, 2)[n - 1]) % nx, 'sub': 0}
         return remote(panel(k, a), panel(k, a), r_send.at[a, n], r_recv.at[k, a], target)
 
     def fwd_copy(k, a):
@@ -111,7 +107,7 @@
         return (sub == 0) & (x != k // nsub)
 
     def far_here(k, a):
-        return (sub == 0) & (x == (k // nsub + far_step(a)) % nx)
+        return (sub == 0) & (x == (k // nsub + far_step(a)) % nx) & (k + 1 < nrows)
 
     def nxt_copy(k, a, d):
         src = pl.ds(pl.multiple_of(blk + (k + 1) // ncols * blk, LANES), blk)
@@ -123,7 +119,7 @@
 
     def send_col(k, h):
         colp[k, half_rows(h)] = work[half_rows(h), own_cols(k)]
-        for d in (1, ncols - 1) + tuple(range(2, ncols - 1)):
+        for d in tuple(range(2, ncols - 1)) + (1, ncols - 1):
             col_copy(k, h, d, d - 1).start()
 
     def send_diag(h):
@@ -164,76 +160,90 @@
             return carry
         lax.fori_loop(0, count // step, body, 0)
 
+    def tile_rows(f, l):
+        return slice(f * SUBL, l * SUBL)
+
+    def close_chunk(k, a):
+        dl = dlo - blk
+        base = a * tiles_per_chunk
+        vals = [work[tile_rows(base + t, base + t + 1), blk:width] for t in range(tiles_per_chunk)]
+        for g in range(tiles_per_chunk):
+            cols = [dl + (base + g) * SUBL + n for n in range(SUBL)]
+            others = [t for t in range(tiles_per_chunk) if t != g]
+            wide = jnp.concatenate([lane_bcast(vals[g], c) for c in cols] + [vals[g]], axis=1)
+            spread = {t: [lane_bcast(vals[t], c) for c in cols] for t in others}
+            for p in range(SUBL):
+                piv, wide = wide[:, :LANES], wide[:, LANES:]
+                wide = jnp.minimum(wide, widen(piv, wide.shape[1]) + jnp.broadcast_to(wide[p:p + 1, :], wide.shape))
+            vals[g] = wide
+            for t in others[g:] + others[:g]:
+                for n in range(SUBL):
+                    vals[t] = jnp.minimum(vals[t], widen(spread[t][n], own + blk) + jnp.broadcast_to(wide[n:n + 1, :], wide.shape))
+        for t, v in enumerate(vals):
+            r = tile_rows(t, t + 1)
+            work[tile_rows(base + t, base + t + 1), blk:width] = v
+            rowp[k, a, r, 0:blk] = v[:, dl:]
+            rowp[k, a, r, blk:width] = v
+
+    def send_chunk(k, a):
+        sends_next = (k + 1 < nrows) & (my_col == (k + 1) % ncols)
+
+        @pl.when(sends_next)
+        def _():
+            nxt_copy(k, a, 1).start()
+        row_copy(k, a, 0).start()
+        row_copy(k, a, 2).start()
+
+        @pl.when(sends_next)
+        def _():
+            for d in range(2, ncols):
+                nxt_copy(k, a, d).start()
+        row_copy(k, a, 1).start()
+
+        @pl.when(k + 1 == nrows)
+        def _():
+            row_copy(k, a, 3).start()
+
+    def relax_by_chunk(a, f, l, step):
+        for t in range(f, l, step):
+            r = tile_rows(t, min(t + step, l))
+            rows = lambda n: work[a * CHUNK + n:a * CHUNK + n + 1, blk:width]
+            work[r, blk:width] = relax(work[r, blk:width], work[r, dlo:width], range(a * CHUNK, (a + 1) * CHUNK), rows)
+
+    def spread_cols(a, f, l):
+        r = tile_rows(f, l)
+        src = work[r, dlo:width]
+        for n in range(CHUNK):
+            spread[n, r, :] = lane_bcast(src, a * CHUNK + n)
+
+    def relax_spread(a, f, l):
+        r = tile_rows(f, l)
+        acc = work[r, blk:width]
+        for n in range(CHUNK):
+            row = work[a * CHUNK + n:a * CHUNK + n + 1, blk:width]
+            acc = jnp.minimum(acc, widen(spread[n, r, :], own + blk) + jnp.broadcast_to(row, acc.shape))
+        work[r, blk:width] = acc
+
     def own_turn(k):
-        lo, hi, dl = blk, width, dlo - blk
-
-        def rows(f, l):
-            return slice(f * SUBL, l * SUBL)
-
-        def in_play(g):
-            return range(g // tiles_per_chunk * tiles_per_chunk, tiles) if g < tiles else range(0)
-
-        def runs(ts):
-            out = []
-            for t in ts:
-                if out and out[-1][1] == t and t - out[-1][0] < 4:
-                    out[-1][1] = t + 1
-                else:
-                    out.append([t, t + 1])
-            return out
-
-        def expand(g, f, l, vals):
-            for n in range(SUBL):
-                lanes[g % 2, n, rows(f, l), :] = lane_bcast(vals, dl + g * SUBL + n)
-
-        def relaxed(g, f, l, cur):
-            acc = work[rows(f, l), lo:hi]
-            for n in range(SUBL):
-                acc = jnp.minimum(acc, widen(lanes[g % 2, n, rows(f, l), :], hi - lo) + jnp.broadcast_to(cur[n:n + 1, :], acc.shape))
-            return acc
-
-        def relax_tiles(g, ts, cur):
-            for f, l in runs(ts):
-                vals = relaxed(g, f, l, cur)
-                work[rows(f, l), lo:hi] = vals
-                if f in in_play(g + 1):
-                    expand(g + 1, f, l, vals)
-
-        work[rows(0, 1), lo:hi] = close_tile(work[rows(0, 1), lo:hi], dl)
-        for f, l in runs(range(1, tiles)):
-            expand(0, f, l, work[rows(f, l), lo:hi])
-        for g in range(tiles):
-            a = g // tiles_per_chunk
-            cur = work[rows(g, g + 1), lo:hi]
-            rest = [t for t in in_play(g) if t not in (g, g + 1)]
-            if (g + 1) % tiles_per_chunk == 0:
-                relax_tiles(g, [t for t in rest if t < g], cur)
-                rest = [t for t in rest if t > g]
-                r = slice(a * CHUNK, (a + 1) * CHUNK)
-                rowp[k, a, :, 0:blk] = work[r, dlo:width]
-                rowp[k, a, :, blk:dlo] = work[r, blk:dlo]
-                rowp[k, a, :, dlo:width] = work[r, dlo:width]
-                @pl.when((k + 1 < nrows) & (my_col == (k + 1) % ncols))
-                def _():
-                    nxt_copy(k, a, 1).start()
-                row_copy(k, a, 0).start()
-                row_copy(k, a, 2).start()
-                @pl.when((k + 1 < nrows) & (my_col == (k + 1) % ncols))
-                def _():
-                    for d in range(2, ncols):
-                        nxt_copy(k, a, d).start()
-                row_copy(k, a, 1).start()
-            if g + 1 < tiles:
-                nxt = relaxed(g, g + 1, g + 2, cur)
-                wide = jnp.concatenate([lane_bcast(nxt, dl + (g + 1) * SUBL + n) for n in range(SUBL)] + [nxt], axis=1)
-                if g in in_play(g + 1):
-                    expand(g + 1, g, g + 1, cur)
-            relax_tiles(g, rest, cur)
-            if g + 1 < tiles:
-                for p in range(SUBL):
-                    piv, wide = wide[:, :LANES], wide[:, LANES:]
-                    wide = jnp.minimum(wide, widen(piv, wide.shape[1]) + jnp.broadcast_to(wide[p:p + 1, :], wide.shape))
-                work[rows(g + 1, g + 2), lo:hi] = wide
+        n = tiles_per_chunk
+
+        close_chunk(k, 0)
+        spread_cols(0, n, 2 * n)
+        send_chunk(k, 0)
+        relax_spread(0, n, 2 * n)
+        close_chunk(k, 1)
+        relax_by_chunk(0, 2 * n, 3 * n, n)
+        spread_cols(1, 2 * n, 3 * n)
+        send_chunk(k, 1)
+        relax_spread(1, 2 * n, 3 * n)
+        close_chunk(k, 2)
+        relax_by_chunk(0, 3 * n, tiles, n)
+        relax_by_chunk(1, 3 * n, tiles, n)
+        spread_cols(2, 3 * n, tiles)
+        send_chunk(k, 2)
+        relax_spread(2, 3 * n, tiles)
+        close_chunk(k, 3)
+        send_chunk(k, 3)
         for a in range(1, nchunk):
             apply_rows(blk, width, dlo, k, a, a * CHUNK, CHUNK)
 
@@ -248,27 +258,7 @@
         def _():
             far_copy(k, a).start()
 
-    def next_turn(k):
-        holder = my_col == (k + 1) % ncols
-        recv_row(k, 0)
-        for h in range(HALVES):
-            recv_col(k, h)
-        recv_diag()
-        for a in range(nchunk):
-            if a > 0:
-                recv_row(k, a)
-
-            @pl.when(holder)
-            def _():
-                rowp[k, a, :, dlo:width] = rowp[k, a, :, own_cols(k + 1)]
-
-            @pl.when(jnp.logical_not(holder))
-            def _():
-                nxt_copy(k, a, 1).wait_recv()
-            apply_rows(0 if a < nchunk - 1 else blk, width, 0, k, a, blk, blk)
-
-    def relax_half(k, a, h, sections, save=False, load=False):
-        r = half_rows(h)
+    def relax_block(k, a, r, sections, save=False, load=False):
         accs = [work[r, c] for c in sections]
         src = work[r, 0:blk]
         for n in range(CHUNK):
@@ -283,8 +273,108 @@
         for acc, c in zip(accs, sections):
             work[r, c] = acc
 
+    first = slice(0, blk)
+
+    def rest(k, b):
+        other = pl.ds(pl.multiple_of(own - b // ncols * blk, LANES), blk)
+        def body(h, carry):
+            for a in range(nchunk):
+                relax_block(k, a, half_rows(h), [other], load=True)
+            return carry
+        lax.fori_loop(0, HALVES, body, 0)
+
+    def next_turn(k):
+        last = nchunk - 1
+
+        def next_rows(a):
+            holder = my_col == (k + 1) % ncols
+
+            @pl.when(holder)
+            def _():
+                rowp[k, a, :, dlo:width] = rowp[k, a, :, own_cols(k + 1)]
+
+            @pl.when(jnp.logical_not(holder))
+            def _():
+                nxt_copy(k, a, 1).wait_recv()
+
+        recv_row(k, 0)
+
+        def spread_last(r):
+            src = work[r, 0:blk]
+            for n in range(last * CHUNK, blk):
+                spread[n, r, :] = lane_bcast(src, n)
+
+        @pl.when(sub >= 0)
+        def _():
+            def body(h, carry):
+                recv_col(k, h)
+                for a in range(last):
+                    if a > 0:
+                        @pl.when(h == 0)
+                        def _():
+                            recv_row(k, a)
+                    relax_block(k, a, half_rows(h), [slice(0, dlo)], save=True)
+                spread_last(half_rows(h))
+                return carry
+            lax.fori_loop(0, HALVES, body, 0)
+        recv_row(k, last)
+        recv_diag()
+        for a in range(last):
+            next_rows(a)
+            relax_block(k, a, slice(0, blk), [slice(dlo, width)], load=True)
+        next_rows(last)
+
+        def finish(h, carry):
+            relax_block(k, last, half_rows(h), [slice(blk, width)], load=True)
+            return carry
+        lax.fori_loop(0, HALVES, finish, 0)
+
+    def second_turn(k):
+        sends_col = my_col == (k + 1) % ncols
+        sends_diag = my_col == (k + 2) % ncols
+        block = jnp.where(sends_col, k + 1, k + 2)
+        recv_row(k, 0)
+
+        def half_turn(h, sections, save):
+            recv_col(k, h)
+            for a in range(nchunk):
+                if a > 0:
+                    @pl.when(h == 0)
+                    def _():
+                        recv_row(k, a)
+                relax_block(k, a, half_rows(h), sections(a), save=save)
+
+        @pl.when(sends_col | sends_diag)
+        def _():
+            def body(h, carry):
+                half_turn(h, lambda a: ([first] if a < nchunk - 1 else []) + [own_cols(block)], True)
+
+                @pl.when(sends_col)
+                def _():
+                    send_col(k + 1, h)
+
+                @pl.when(sends_diag)
+                def _():
+                    send_diag(h)
+                return carry
+            lax.fori_loop(0, HALVES, body, 0)
+            rest(k, block)
+
+        @pl.when(jnp.logical_not(sends_col | sends_diag))
+        def _():
+            def body(h, carry):
+                half_turn(h, lambda a: [slice(0 if a < nchunk - 1 else blk, dlo)], False)
+                return carry
+            lax.fori_loop(0, HALVES, body, 0)
+
+    def last_turn(k):
+        for h in range(HALVES):
+            recv_col(k, h)
+        for a in range(nchunk):
+            recv_row(k, a)
+            relax_block(k, a, slice(0, blk), [slice(0 if a < nchunk - 1 else blk, dlo)])
+
     def other_turn(k):
-        first = slice(0, blk)
         holder = (k + 1 < nrows) & (my_col == (k + 1) % ncols)
         recv_row(k, 0)
 
@@ -297,18 +387,11 @@
                         @pl.when(h == 0)
                         def _():
                             recv_row(k, a)
-                    secs = [first] if a < nchunk - 1 else []
-                    relax_half(k, a, h, secs + [own_cols(k + 1)], save=True)
+                    relax_block(k, a, half_rows(h), ([first] if a < nchunk - 1 else []) + [own_cols(k + 1)], save=True)
                 send_col(k + 1, h)
                 return carry
             lax.fori_loop(0, HALVES, body, 0)
-
-            other = pl.ds(pl.multiple_of(own - (k + 1) // ncols * blk, LANES), blk)
-            def rest(h, carry):
-                for a in range(nchunk):
-                    relax_half(k, a, h, [other], load=True)
-                return carry
-            lax.fori_loop(0, HALVES, rest, 0)
+            rest(k, k + 1)
 
         @pl.when(jnp.logical_not(holder))
         def _():
@@ -319,11 +402,7 @@
                         @pl.when(h == 0)
                         def _():
                             recv_row(k, a)
-                    relax_half(k, a, h, [slice(0 if a < nchunk - 1 else blk, dlo)])
-
-                @pl.when((my_row == k + 2) & (my_col == my_row % ncols))
-                def _():
-                    send_diag(h)
+                    relax_block(k, a, half_rows(h), [slice(0 if a < nchunk - 1 else blk, dlo)])
                 return carry
             lax.fori_loop(0, HALVES, body, 0)
 
@@ -344,9 +423,17 @@
         def _():
             next_turn(k)
 
-        @pl.when((my_row != k) & (my_row != k + 1))
+        @pl.when(my_row == k + 2)
+        def _():
+            second_turn(k)
+
+        @pl.when(((my_row < k) & (k + 1 < nrows)) | (my_row > k + 2))
         def _():
             other_turn(k)
+
+        @pl.when((my_row < k) & (k + 1 == nrows))
+        def _():
+            last_turn(k)
         return carry
 
     lax.fori_loop(0, nrows, round_body, 0)
@@ -377,8 +464,12 @@
         return carry
     lax.fori_loop(0, nrows, drain, 0)
     for a in range(nchunk):
-        for n in range(nx - 1):
+        for n in range(3):
             row_copy(my_row, a, n).wait_send()
+
+        @pl.when(my_row + 1 == nrows)
+        def _():
+            row_copy(my_row, a, 3).wait_send()
 
         @pl.when((my_row + 1 < nrows) & (my_col == (my_row + 1) % ncols))
         def _():
@@ -407,12 +498,12 @@
             out_specs=pl.BlockSpec(memory_space=pl.ANY),
             scratch_shapes=[
                 vmem(blk, own + 2 * blk), vmem(blk, blk), vmem(nrows, blk, blk),
-                vmem(nrows, nchunk, CHUNK, own + 2 * blk), vmem(2, SUBL, blk, LANES), vmem(blk, blk, LANES), dma((1,)),
+                vmem(nrows, nchunk, CHUNK, own + 2 * blk), vmem(blk, blk, LANES), dma((1,)),
                 dma((nrows, HALVES, ncols - 1)), dma((nrows, HALVES)), dma((HALVES, ncols - 1)), dma((HALVES,)),
-                dma((nchunk, nx - 1)), dma((nrows, nchunk)), dma((nrows, nchunk, 2)),
+                dma((nchunk, 4)), dma((nrows, nchunk)), dma((nrows, nchunk, 2)),
                 dma((nchunk, ncols - 1)), dma((nchunk,)),
             ],
-            compiler_params=pltpu.CompilerParams(collective_id=0, has_side_effects=True),
+            compiler_params=pltpu.CompilerParams(collective_id=0, has_side_effects=True, vmem_limit_bytes=16 * 2**20),
         )(local)
 
     return jax.shard_map(local_run, mesh=mesh, in_specs=(dist_spec,), out_specs=dist_spec, check_vma=False)

time: 83.5 us -> 81.3 us (0.974)
  the two profiles are of different devices: /device:TPU:99 before, /device:TPU:97 now
where the time goes in v3:
time: 81.3 us; the launch traced here: 79.7 us
  Pallas kernels  78.1 us (96%)
  local copies, waits for them, and re-layouts  1.56 us (2%)
    pallas_call x1, Pallas kernels, local_run(): pl.pallas_call(functools.partial(kernel, nrows, ncols, nsub, blk), out_sh...  78.1 us

profile of v3, /device:TPU:97, one launch (start us, length us, event | category | flops | bytes accessed | tf_op | source)
XLA Modules:
  0.0 79.7 jit_solution(5991475940778649609)
XLA Ops:
  0.0 0.0 copy-start
  0.0 0.9 %copy-done = f32[1,128,256]{2,1,0:T(8,128)S(1)} copy-done((f32[1,128,256]{2,1,0:T(8,128)S(1)}, f32[1,128,256]{2,1,0:T(8,128)}, u32[]{:S(2)}) %copy-start) | copy-done | bytes 131096
  0.9 78.1 %shard_map.17 = f32[1,128,256]{2,1,0:T(8,128)S(1)} custom-call(f32[1,128,256]{2,1,0:T(8,128)S(1)} %copy-done), custom_call_target="tpu_custom_call" | custom-call | tf_op jit(solution)/shard_map/pallas_call | solution.py:494
  79.0 0.7 copy.3
Async XLA Ops:
  0.0 0.9 %copy-start = (f32[1,128,256]{2,1,0:T(8,128)S(1)}, f32[1,128,256]{2,1,0:T(8,128)}, u32[]{:S(2)}) copy-start(f32[1,128,256]{2,1,0:T(8,128)} %in_ref.1) | copy-start | bytes 393220

commit v4 on v3

--- a/solution.py
+++ b/solution.py
@@ -10,6 +10,8 @@
 SUBL = 8
 LANES = 128
 CHUNK = 32
+PAIRS = CHUNK // 2
+STEP = 64
 HALVES = 2
 FULL = False
 
@@ -26,6 +28,24 @@
 
 def widen(x, width):
     return jnp.concatenate([x] * (width // LANES), axis=1)
+
+
+def lane_id(rows):
+    return lax.broadcasted_iota(jnp.int32, (rows, LANES), 1)
+
+
+def pair_bcast(tile, lanes):
+    return jnp.take_along_axis(tile, lanes, axis=1, mode='promise_in_bounds')
+
+
+def pair_lanes(rows):
+    return jnp.where(lane_id(rows) < LANES // 2, 0, PAIRS)
+
+
+def pack_rows(block):
+    low = lane_id(PAIRS) < LANES // 2
+    turned = pltpu.roll(block, LANES // 2, 1)
+    return jnp.where(low, block[:PAIRS], turned[PAIRS:]), jnp.where(low, turned[:PAIRS], block[PAIRS:])
 
 
 def kernel(nrows, ncols, nsub, blk, in_ref, out_ref, work, diag_in, colp, rowp, spread, io_sem,
@@ -150,15 +170,6 @@
     def _():
         for h in range(HALVES):
             send_col(0, h)
-
-    def apply_rows(lo, hi, lane_lo, k, a, count, step):
-        def body(it, carry):
-            r = pl.ds(pl.multiple_of(it * step, step), step)
-            rows = lambda n: rowp[k, a, n:n + 1, lo:hi]
-            src = work[r, lane_lo:lane_lo + blk]
-            work[r, lo:hi] = relax(work[r, lo:hi], src, [a * CHUNK + l for l in range(CHUNK)], rows)
-            return carry
-        lax.fori_loop(0, count // step, body, 0)
 
     def tile_rows(f, l):
         return slice(f * SUBL, l * SUBL)
@@ -180,10 +191,14 @@
                 for n in range(SUBL):
                     vals[t] = jnp.minimum(vals[t], widen(spread[t][n], own + blk) + jnp.broadcast_to(wide[n:n + 1, :], wide.shape))
         for t, v in enumerate(vals):
-            r = tile_rows(t, t + 1)
             work[tile_rows(base + t, base + t + 1), blk:width] = v
-            rowp[k, a, r, 0:blk] = v[:, dl:]
-            rowp[k, a, r, blk:width] = v
+        for c in range(0, own + blk, LANES):
+            packed = pack_rows(jnp.concatenate([v[:, c:c + LANES] for v in vals], axis=0))
+            for n, v in enumerate(packed):
+                r = slice(n * PAIRS, (n + 1) * PAIRS)
+                rowp[k, a, r, blk + c:blk + c + LANES] = v
+                if c == dl:
+                    rowp[k, a, r, 0:blk] = v
 
     def send_chunk(k, a):
         sends_next = (k + 1 < nrows) & (my_col == (k + 1) % ncols)
@@ -245,7 +260,12 @@
         close_chunk(k, 3)
         send_chunk(k, 3)
         for a in range(1, nchunk):
-            apply_rows(blk, width, dlo, k, a, a * CHUNK, CHUNK)
+            def body(it, carry):
+                r = pl.ds(pl.multiple_of(it * CHUNK, CHUNK), CHUNK)
+                rows = lambda n: work[a * CHUNK + n:a * CHUNK + n + 1, blk:width]
+                work[r, blk:width] = relax(work[r, blk:width], work[r, dlo:width], range(a * CHUNK, (a + 1) * CHUNK), rows)
+                return carry
+            lax.fori_loop(0, a, body, 0)
 
     def recv_row(k, a):
         fwd_copy(k, a).wait_recv()
@@ -258,20 +278,32 @@
         def _():
             far_copy(k, a).start()
 
-    def relax_block(k, a, r, sections, save=False, load=False):
-        accs = [work[r, c] for c in sections]
-        src = work[r, 0:blk]
-        for n in range(CHUNK):
-            if load:
-                wide = spread[a * CHUNK + n, r, :]
-            else:
-                wide = lane_bcast(src, a * CHUNK + n)
-            if save:
-                spread[a * CHUNK + n, r, :] = wide
-            accs = [jnp.minimum(acc, widen(wide, acc.shape[1]) + jnp.broadcast_to(rowp[k, a, n:n + 1, c], acc.shape))
-                    for acc, c in zip(accs, sections)]
-        for acc, c in zip(accs, sections):
-            work[r, c] = acc
+    def relax_block(k, a, start, count, sections, save=False, load=False):
+        low = lane_id(STEP) < LANES // 2
+        pairs = pair_lanes(STEP)
+        sizes = [c.size if isinstance(c, pl.Slice) else c.stop - c.start for c in sections]
+        for i in range(count // STEP):
+            r = pl.ds(pl.multiple_of(start + i * STEP, STEP), STEP)
+            src = None if load else work[r, 0:blk]
+            accs = [None] * len(sections)
+            for n in range(PAIRS):
+                if load:
+                    wide = spread[a * PAIRS + n, r, :]
+                else:
+                    wide = pair_bcast(src, pairs + (a * CHUNK + n))
+                if save:
+                    spread[a * PAIRS + n, r, :] = wide
+                for c, (cols, size) in enumerate(zip(sections, sizes)):
+                    reps = widen(wide, size)
+                    new = [reps + jnp.broadcast_to(rowp[k, a, m:m + 1, cols], reps.shape) for m in (n, n + PAIRS)]
+                    accs[c] = new if n == 0 else [jnp.minimum(x, y) for x, y in zip(accs[c], new)]
+            for (lower, upper), cols in zip(accs, sections):
+                parts = []
+                for b in range(0, lower.shape[1], LANES):
+                    x, y = lower[:, b:b + LANES], upper[:, b:b + LANES]
+                    parts.append(jnp.minimum(jnp.where(low, x, y), pltpu.roll(jnp.where(low, y, x), LANES // 2, 1)))
+                work[r, cols] = jnp.minimum(work[r, cols], jnp.concatenate(parts, axis=1))
+
 
     first = slice(0, blk)
 
@@ -279,7 +311,7 @@
         other = pl.ds(pl.multiple_of(own - b // ncols * blk, LANES), blk)
         def body(h, carry):
             for a in range(nchunk):
-                relax_block(k, a, half_rows(h), [other], load=True)
+                relax_block(k, a, h * half, half, [other], load=True)
             return carry
         lax.fori_loop(0, HALVES, body, 0)
 
@@ -299,10 +331,11 @@
 
         recv_row(k, 0)
 
-        def spread_last(r):
-            src = work[r, 0:blk]
-            for n in range(last * CHUNK, blk):
-                spread[n, r, :] = lane_bcast(src, n)
+        def spread_last(h):
+            src = work[half_rows(h), 0:blk]
+            pairs = pair_lanes(half)
+            for n in range(PAIRS):
+                spread[last * PAIRS + n, half_rows(h), :] = pair_bcast(src, pairs + (last * CHUNK + n))
 
         @pl.when(sub >= 0)
         def _():
@@ -313,19 +346,19 @@
                         @pl.when(h == 0)
                         def _():
                             recv_row(k, a)
-                    relax_block(k, a, half_rows(h), [slice(0, dlo)], save=True)
-                spread_last(half_rows(h))
+                    relax_block(k, a, h * half, half, [slice(0, dlo)], save=True)
+                spread_last(h)
                 return carry
             lax.fori_loop(0, HALVES, body, 0)
         recv_row(k, last)
         recv_diag()
         for a in range(last):
             next_rows(a)
-            relax_block(k, a, slice(0, blk), [slice(dlo, width)], load=True)
+            relax_block(k, a, 0, blk, [slice(dlo, width)], load=True)
         next_rows(last)
 
         def finish(h, carry):
-            relax_block(k, last, half_rows(h), [slice(blk, width)], load=True)
+            relax_block(k, last, h * half, half, [slice(blk, width)], load=True)
             return carry
         lax.fori_loop(0, HALVES, finish, 0)
 
@@ -342,7 +375,7 @@
                     @pl.when(h == 0)
                     def _():
                         recv_row(k, a)
-                relax_block(k, a, half_rows(h), sections(a), save=save)
+                relax_block(k, a, h * half, half, sections(a), save=save)
 
         @pl.when(sends_col | sends_diag)
         def _():
@@ -372,7 +405,7 @@
             recv_col(k, h)
         for a in range(nchunk):
             recv_row(k, a)
-            relax_block(k, a, slice(0, blk), [slice(0 if a < nchunk - 1 else blk, dlo)])
+            relax_block(k, a, 0, blk, [slice(0 if a < nchunk - 1 else blk, dlo)])
 
     def other_turn(k):
         holder = (k + 1 < nrows) & (my_col == (k + 1) % ncols)
@@ -387,7 +420,7 @@
                         @pl.when(h == 0)
                         def _():
                             recv_row(k, a)
-                    relax_block(k, a, half_rows(h), ([first] if a < nchunk - 1 else []) + [own_cols(k + 1)], save=True)
+                    relax_block(k, a, h * half, half, ([first] if a < nchunk - 1 else []) + [own_cols(k + 1)], save=True)
                 send_col(k + 1, h)
                 return carry
             lax.fori_loop(0, HALVES, body, 0)
@@ -402,7 +435,7 @@
                         @pl.when(h == 0)
                         def _():
                             recv_row(k, a)
-                    relax_block(k, a, half_rows(h), [slice(0 if a < nchunk - 1 else blk, dlo)])
+                    relax_block(k, a, h * half, half, [slice(0 if a < nchunk - 1 else blk, dlo)])
                 return carry
             lax.fori_loop(0, HALVES, body, 0)
 

time: 81.3 us -> 79.2 us (0.974)
  Pallas kernels: 78.1 us -> 76.2 us
    pallas_call x1, Pallas kernels: 78.1 us -> 76.2 us  [local_run(): pl.pallas_call(functools.partial(kernel, nrows, ncols, nsub, blk), out_sh...]
where the time goes in v4:
time: 79.2 us; the launch traced here: 77.7 us
  Pallas kernels  76.2 us (96%)
  local copies, waits for them, and re-layouts  1.56 us (2%)
    pallas_call x1, Pallas kernels, local_run(): pl.pallas_call(functools.partial(kernel, nrows, ncols, nsub, blk), out_sh...  76.2 us

profile of v4, /device:TPU:97, one launch (start us, length us, event | category | flops | bytes accessed | tf_op | source)
XLA Modules:
  0.0 77.7 jit_solution(14999384744138473772)
XLA Ops:
  0.0 0.0 copy-start
  0.0 0.9 %copy-done = f32[1,128,256]{2,1,0:T(8,128)S(1)} copy-done((f32[1,128,256]{2,1,0:T(8,128)S(1)}, f32[1,128,256]{2,1,0:T(8,128)}, u32[]{:S(2)}) %copy-start) | copy-done | bytes 131096
  0.9 76.2 %shard_map.17 = f32[1,128,256]{2,1,0:T(8,128)S(1)} custom-call(f32[1,128,256]{2,1,0:T(8,128)S(1)} %copy-done), custom_call_target="tpu_custom_call" | custom-call | tf_op jit(solution)/shard_map/pallas_call | solution.py:527
  77.1 0.7 copy.3
Async XLA Ops:
  0.0 0.9 %copy-start = (f32[1,128,256]{2,1,0:T(8,128)S(1)}, f32[1,128,256]{2,1,0:T(8,128)}, u32[]{:S(2)}) copy-start(f32[1,128,256]{2,1,0:T(8,128)} %in_ref.1) | copy-start | bytes 393220

commit v5 on v4

--- a/solution.py
+++ b/solution.py
@@ -348,9 +348,16 @@
                             recv_row(k, a)
                     relax_block(k, a, h * half, half, [slice(0, dlo)], save=True)
                 spread_last(h)
+
+                @pl.when((h == 0) & (sub == 0))
+                def _():
+                    recv_row(k, last)
                 return carry
             lax.fori_loop(0, HALVES, body, 0)
-        recv_row(k, last)
+
+        @pl.when(sub > 0)
+        def _():
+            recv_row(k, last)
         recv_diag()
         for a in range(last):
             next_rows(a)
@@ -400,12 +407,23 @@
                 return carry
             lax.fori_loop(0, HALVES, body, 0)
 
+    def store_half(h):
+        return pltpu.make_async_copy(work.at[half_rows(h), blk:dlo], out_ref.at[0, half_rows(h)], io_sem.at[h])
+
     def last_turn(k):
-        for h in range(HALVES):
+        recv_row(k, 0)
+
+        def body(h, carry):
             recv_col(k, h)
-        for a in range(nchunk):
-            recv_row(k, a)
-            relax_block(k, a, 0, blk, [slice(0 if a < nchunk - 1 else blk, dlo)])
+            for a in range(nchunk):
+                if a > 0:
+                    @pl.when(h == 0)
+                    def _():
+                        recv_row(k, a)
+                relax_block(k, a, h * half, half, [slice(0 if a < nchunk - 1 else blk, dlo)])
+            store_half(h).start()
+            return carry
+        lax.fori_loop(0, HALVES, body, 0)
 
     def other_turn(k):
         holder = (k + 1 < nrows) & (my_col == (k + 1) % ncols)
@@ -471,8 +489,10 @@
 
     lax.fori_loop(0, nrows, round_body, 0)
 
-    store_out = pltpu.make_async_copy(work.at[:, blk:dlo], out_ref.at[0], io_sem.at[0])
-    store_out.start()
+    @pl.when(my_row + 1 == nrows)
+    def _():
+        for h in range(HALVES):
+            store_half(h).start()
 
     @pl.when(my_col == my_row % ncols)
     def _():
@@ -508,7 +528,8 @@
         def _():
             for d in range(1, ncols):
                 nxt_copy(my_row, a, d).wait_send()
-    store_out.wait()
+    for h in range(HALVES):
+        store_half(h).wait()
 
 
 def solution(mesh):
@@ -531,7 +552,7 @@
             out_specs=pl.BlockSpec(memory_space=pl.ANY),
             scratch_shapes=[
                 vmem(blk, own + 2 * blk), vmem(blk, blk), vmem(nrows, blk, blk),
-                vmem(nrows, nchunk, CHUNK, own + 2 * blk), vmem(blk, blk, LANES), dma((1,)),
+                vmem(nrows, nchunk, CHUNK, own + 2 * blk), vmem(blk, blk, LANES), dma((HALVES,)),
                 dma((nrows, HALVES, ncols - 1)), dma((nrows, HALVES)), dma((HALVES, ncols - 1)), dma((HALVES,)),
                 dma((nchunk, 4)), dma((nrows, nchunk)), dma((nrows, nchunk, 2)),
                 dma((nchunk, ncols - 1)), dma((nchunk,)),

time: 79.2 us -> 77.3 us (0.976); the launches traced: 77.7 us -> 77.2 us
  no operation moved by 1% of the time
where the time goes in v5:
time: 77.3 us; the launch traced here: 77.2 us
  Pallas kernels  75.7 us (98%)
  local copies, waits for them, and re-layouts  1.56 us (2%)
    pallas_call x1, Pallas kernels, local_run(): pl.pallas_call(functools.partial(kernel, nrows, ncols, nsub, blk), out_sh...  75.7 us
    unnamed x3, local copies, waits for them, and re-layouts  1.56 us

profile of v5, /device:TPU:97, one launch (start us, length us, event | category | flops | bytes accessed | tf_op | source)
XLA Modules:
  0.0 77.2 jit_solution(16125423224308845352)
XLA Ops:
  0.0 0.0 copy-start
  0.0 0.9 %copy-done = f32[1,128,256]{2,1,0:T(8,128)S(1)} copy-done((f32[1,128,256]{2,1,0:T(8,128)S(1)}, f32[1,128,256]{2,1,0:T(8,128)}, u32[]{:S(2)}) %copy-start) | copy-done | bytes 131096
  0.9 75.7 %shard_map.17 = f32[1,128,256]{2,1,0:T(8,128)S(1)} custom-call(f32[1,128,256]{2,1,0:T(8,128)S(1)} %copy-done), custom_call_target="tpu_custom_call" | custom-call | tf_op jit(solution)/shard_map/pallas_call | solution.py:548
  76.6 0.7 copy.3
Async XLA Ops:
  0.0 0.9 %copy-start = (f32[1,128,256]{2,1,0:T(8,128)S(1)}, f32[1,128,256]{2,1,0:T(8,128)}, u32[]{:S(2)}) copy-start(f32[1,128,256]{2,1,0:T(8,128)} %in_ref.1) | copy-start | bytes 393220

commit v6 on v5

--- a/solution.py
+++ b/solution.py
@@ -278,7 +278,8 @@
         def _():
             far_copy(k, a).start()
 
-    def relax_block(k, a, start, count, sections, save=False, load=False):
+    def relax_block(k, chunks, start, count, sections, save=False, load=False):
+        chunks = chunks if isinstance(chunks, tuple) else (chunks,)
         low = lane_id(STEP) < LANES // 2
         pairs = pair_lanes(STEP)
         sizes = [c.size if isinstance(c, pl.Slice) else c.stop - c.start for c in sections]
@@ -286,7 +287,7 @@
             r = pl.ds(pl.multiple_of(start + i * STEP, STEP), STEP)
             src = None if load else work[r, 0:blk]
             accs = [None] * len(sections)
-            for n in range(PAIRS):
+            for a, n in [(a, n) for a in chunks for n in range(PAIRS)]:
                 if load:
                     wide = spread[a * PAIRS + n, r, :]
                 else:
@@ -296,7 +297,7 @@
                 for c, (cols, size) in enumerate(zip(sections, sizes)):
                     reps = widen(wide, size)
                     new = [reps + jnp.broadcast_to(rowp[k, a, m:m + 1, cols], reps.shape) for m in (n, n + PAIRS)]
-                    accs[c] = new if n == 0 else [jnp.minimum(x, y) for x, y in zip(accs[c], new)]
+                    accs[c] = new if accs[c] is None else [jnp.minimum(x, y) for x, y in zip(accs[c], new)]
             for (lower, upper), cols in zip(accs, sections):
                 parts = []
                 for b in range(0, lower.shape[1], LANES):
@@ -310,8 +311,7 @@
     def rest(k, b):
         other = pl.ds(pl.multiple_of(own - b // ncols * blk, LANES), blk)
         def body(h, carry):
-            for a in range(nchunk):
-                relax_block(k, a, h * half, half, [other], load=True)
+            relax_block(k, tuple(range(nchunk)), h * half, half, [other], load=True)
             return carry
         lax.fori_loop(0, HALVES, body, 0)
 
@@ -358,16 +358,17 @@
         @pl.when(sub > 0)
         def _():
             recv_row(k, last)
+
+        def finish(h, carry):
+            relax_block(k, last, h * half, half, [slice(blk, dlo)], load=True)
+            return carry
+        lax.fori_loop(0, HALVES, finish, 0)
         recv_diag()
         for a in range(last):
             next_rows(a)
-            relax_block(k, a, 0, blk, [slice(dlo, width)], load=True)
+        relax_block(k, tuple(range(last)), 0, blk, [slice(dlo, width)], load=True)
         next_rows(last)
-
-        def finish(h, carry):
-            relax_block(k, last, h * half, half, [slice(blk, width)], load=True)
-            return carry
-        lax.fori_loop(0, HALVES, finish, 0)
+        relax_block(k, last, 0, blk, [slice(dlo, width)], load=True)
 
     def second_turn(k):
         sends_col = my_col == (k + 1) % ncols

time: 77.3 us -> 76.7 us (level)
  no operation moved by 1% of the time
where the time goes in v6:
time: 76.7 us; the launch traced here: 76.6 us
  Pallas kernels  75 us (98%)
  local copies, waits for them, and re-layouts  1.56 us (2%)
    pallas_call x1, Pallas kernels, local_run(): pl.pallas_call(functools.partial(kernel, nrows, ncols, nsub, blk), out_sh...  75 us
    unnamed x3, local copies, waits for them, and re-layouts  1.56 us

profile of v6, /device:TPU:97, one launch (start us, length us, event | category | flops | bytes accessed | tf_op | source)
XLA Modules:
  0.0 76.6 jit_solution(6503929084983314987)
XLA Ops:
  0.0 0.0 copy-start
  0.0 0.9 %copy-done = f32[1,128,256]{2,1,0:T(8,128)S(1)} copy-done((f32[1,128,256]{2,1,0:T(8,128)S(1)}, f32[1,128,256]{2,1,0:T(8,128)}, u32[]{:S(2)}) %copy-start) | copy-done | bytes 131096
  0.9 75.0 %shard_map.17 = f32[1,128,256]{2,1,0:T(8,128)S(1)} custom-call(f32[1,128,256]{2,1,0:T(8,128)S(1)} %copy-done), custom_call_target="tpu_custom_call" | custom-call | tf_op jit(solution)/shard_map/pallas_call | solution.py:549
  75.9 0.7 copy.3
Async XLA Ops:
  0.0 0.9 %copy-start = (f32[1,128,256]{2,1,0:T(8,128)S(1)}, f32[1,128,256]{2,1,0:T(8,128)}, u32[]{:S(2)}) copy-start(f32[1,128,256]{2,1,0:T(8,128)} %in_ref.1) | copy-start | bytes 393220

commit v7 on v6

--- a/solution.py
+++ b/solution.py
@@ -203,17 +203,14 @@
     def send_chunk(k, a):
         sends_next = (k + 1 < nrows) & (my_col == (k + 1) % ncols)
 
-        @pl.when(sends_next)
-        def _():
-            nxt_copy(k, a, 1).start()
         row_copy(k, a, 0).start()
         row_copy(k, a, 2).start()
+        row_copy(k, a, 1).start()
 
         @pl.when(sends_next)
         def _():
-            for d in range(2, ncols):
+            for d in tuple(range(2, ncols - 1)) + (1, ncols - 1):
                 nxt_copy(k, a, d).start()
-        row_copy(k, a, 1).start()
 
         @pl.when(k + 1 == nrows)
         def _():

time: 76.7 us -> 76.2 us (level)
  no operation moved by 1% of the time
where the time goes in v7:
time: 76.2 us; the launch traced here: 76.1 us
  Pallas kernels  74.5 us (98%)
  local copies, waits for them, and re-layouts  1.56 us (2%)
    pallas_call x1, Pallas kernels, local_run(): pl.pallas_call(functools.partial(kernel, nrows, ncols, nsub, blk), out_sh...  74.5 us
    unnamed x3, local copies, waits for them, and re-layouts  1.56 us

profile of v7, /device:TPU:97, one launch (start us, length us, event | category | flops | bytes accessed | tf_op | source)
XLA Modules:
  0.0 76.1 jit_solution(13808296722779797674)
XLA Ops:
  0.0 0.0 copy-start
  0.0 0.9 %copy-done = f32[1,128,256]{2,1,0:T(8,128)S(1)} copy-done((f32[1,128,256]{2,1,0:T(8,128)S(1)}, f32[1,128,256]{2,1,0:T(8,128)}, u32[]{:S(2)}) %copy-start) | copy-done | bytes 131096
  0.9 74.5 %shard_map.17 = f32[1,128,256]{2,1,0:T(8,128)S(1)} custom-call(f32[1,128,256]{2,1,0:T(8,128)S(1)} %copy-done), custom_call_target="tpu_custom_call" | custom-call | tf_op jit(solution)/shard_map/pallas_call | solution.py:546
  75.4 0.7 copy.3
Async XLA Ops:
  0.0 0.9 %copy-start = (f32[1,128,256]{2,1,0:T(8,128)S(1)}, f32[1,128,256]{2,1,0:T(8,128)}, u32[]{:S(2)}) copy-start(f32[1,128,256]{2,1,0:T(8,128)} %in_ref.1) | copy-start | bytes 393220

commit v8 on v7

--- a/solution.py
+++ b/solution.py
@@ -246,10 +246,10 @@
         close_chunk(k, 1)
         relax_by_chunk(0, 2 * n, 3 * n, n)
         spread_cols(1, 2 * n, 3 * n)
+        relax_by_chunk(0, 3 * n, tiles, n)
         send_chunk(k, 1)
         relax_spread(1, 2 * n, 3 * n)
         close_chunk(k, 2)
-        relax_by_chunk(0, 3 * n, tiles, n)
         relax_by_chunk(1, 3 * n, tiles, n)
         spread_cols(2, 3 * n, tiles)
         send_chunk(k, 2)

time: 76.2 us -> 75.9 us (level)
  no operation moved by 1% of the time
where the time goes in v8:
time: 75.9 us; the launch traced here: 75.8 us
  Pallas kernels  74.3 us (98%)
  local copies, waits for them, and re-layouts  1.56 us (2%)
    pallas_call x1, Pallas kernels, local_run(): pl.pallas_call(functools.partial(kernel, nrows, ncols, nsub, blk), out_sh...  74.3 us
    unnamed x3, local copies, waits for them, and re-layouts  1.56 us

profile of v8, /device:TPU:97, one launch (start us, length us, event | category | flops | bytes accessed | tf_op | source)
XLA Modules:
  0.0 75.8 jit_solution(10322627135827369162)
XLA Ops:
  0.0 0.0 copy-start
  0.0 0.9 %copy-done = f32[1,128,256]{2,1,0:T(8,128)S(1)} copy-done((f32[1,128,256]{2,1,0:T(8,128)S(1)}, f32[1,128,256]{2,1,0:T(8,128)}, u32[]{:S(2)}) %copy-start) | copy-done | bytes 131096
  0.9 74.3 %shard_map.17 = f32[1,128,256]{2,1,0:T(8,128)S(1)} custom-call(f32[1,128,256]{2,1,0:T(8,128)S(1)} %copy-done), custom_call_target="tpu_custom_call" | custom-call | tf_op jit(solution)/shard_map/pallas_call | solution.py:546
  75.2 0.7 copy.3
Async XLA Ops:
  0.0 0.9 %copy-start = (f32[1,128,256]{2,1,0:T(8,128)S(1)}, f32[1,128,256]{2,1,0:T(8,128)}, u32[]{:S(2)}) copy-start(f32[1,128,256]{2,1,0:T(8,128)} %in_ref.1) | copy-start | bytes 393220
